TPU v7x, 8 devices: a whole 2x2x1 slice. The times are simulated.
8 devices in a mesh: dp: 1 (over z), tp: 8 (over y, x, core).
Axes of the slice: x: 2, y: 2, z: 1, core: 2. Of those that a mesh axis runs over, the one named last changes fastest.
Arguments:
- x_norm: bfloat16 [4096, 4096], P(('dp', 'tp'))
- w_gate: bfloat16 [4096, 14336], P(None, 'tp')
- w_up: bfloat16 [4096, 14336], P(None, 'tp')
- w_down: bfloat16 [14336, 4096], P('tp')
- u_gate: bfloat16 [4096, 14336], P('dp', 'tp')
- u_up: bfloat16 [4096, 14336], P('dp', 'tp')
- grad_out: bfloat16 [4096, 4096], P(('dp', 'tp'))
Outputs:
- output 1: bfloat16 [4096, 4096], P(('dp', 'tp'))
- output 2: float32 [4096, 14336], P('dp', 'tp')
- output 3: float32 [4096, 14336], P('dp', 'tp')
- output 4: float32 [14336, 4096], P(('dp', 'tp'))
All inputs are finite; a program needn't handle non-finite values.
Results may differ from a plain program's by a relative error of at most 0.0104291.
Values are sent between devices in bfloat16 or wider.
A program may use at most 1 GiB of HBM per device.

v0:
```python
import jax
import jax.numpy as jnp
from jax import lax
from jax.experimental import pallas as pl
from jax.experimental.pallas import tpu as pltpu
from jax.sharding import PartitionSpec as P


F32 = jnp.float32
BF16 = jnp.bfloat16
CHUNKS = 2
NT = (((1,), (1,)), ((), ()))
NN = (((1,), (0,)), ((), ()))
VMEM_LIMIT = 60 * 1024 * 1024


def _call(body, args, *, flops, nbytes, grid, in_specs, out_specs, out_shape, place=None, deps=(), aliases=None):
    n_in, n_dep, first = len(in_specs), len(deps), 0 if place is None else 1

    def kernel(*refs):
        body(*refs[first:first + n_in], *refs[first + n_in + n_dep:])

    return pl.pallas_call(
        kernel,
        grid_spec=pltpu.PrefetchScalarGridSpec(
            num_scalar_prefetch=first, grid=grid,
            in_specs=list(in_specs) + [pl.BlockSpec(memory_space=pl.ANY)] * n_dep, out_specs=out_specs),
        out_shape=out_shape,
        input_output_aliases=aliases or {},
        compiler_params=pltpu.CompilerParams(vmem_limit_bytes=VMEM_LIMIT),
        cost_estimate=pl.CostEstimate(flops=flops, bytes_accessed=nbytes, transcendentals=0),
    )(*([] if place is None else [place]), *args, *deps)


def _fixed(shape, *index):
    def at(i, *place):
        return tuple(place[0][int(e[1:])] if isinstance(e, str) else e for e in index)

    return pl.BlockSpec(shape, at, pipeline_mode=pl.Buffered(1))


def _along(shape, axis, *index, offset=0):
    def at(i, *place):
        out = [place[0][int(e[1:])] if isinstance(e, str) else e for e in index]
        out[axis] = i + offset
        return tuple(out)

    return pl.BlockSpec(shape, at)


def _value(ref):
    return ref[...].reshape(ref.shape[-2:]) if len(ref.shape) < 4 or ref.shape[1] == 1 else ref[...].reshape(-1, ref.shape[-1])


def _rows_of(refs):
    vals = [_value(r) for r in refs]
    return vals[0] if len(vals) == 1 else jnp.concatenate(vals, axis=0)


def _z_body(ug_ref, uu_ref, *rest):
    _, both, rows, width = ug_ref.shape
    gate = ug_ref[...].reshape(both * rows, width).astype(F32)
    z = gate * jax.nn.sigmoid(gate) * uu_ref[...].reshape(both * rows, width).astype(F32)
    rest[-1][...] = z.astype(BF16).T


def _z_transposed(place, ug4, uu4, first, count, old, deps):
    group, both, rows, width = ug4.shape
    tok = both * rows
    spec = pl.BlockSpec((1, both, rows, width), lambda i, p: (p[i + first], 0, 0, 0))
    args = [ug4, uu4] + ([] if old is None else [old])
    return _call(
        _z_body, args, flops=count * tok * width * 8, nbytes=count * tok * width * 6, place=place, deps=deps,
        grid=(count,), in_specs=[spec, spec] + [pl.BlockSpec(memory_space=pl.ANY)] * (len(args) - 2),
        out_specs=pl.BlockSpec((width, tok), lambda i, p: (0, i + first)),
        out_shape=jax.ShapeDtypeStruct((width, group * tok), BF16),
        aliases=None if old is None else {3: 0})


def _mid_grads(place, units, wd, ug4, uu4, lead, old, deps, step=256):
    width, hidden = wd.shape
    rows = ug4.shape[2]
    n = len(units)
    pieces = [p for ps, _, _ in units for p in ps]
    counts = [len(ps) for ps, _, _ in units]

    def body(*refs):
        dy_refs, refs = refs[:len(pieces)], refs[len(pieces):]
        wd_ref, ug_refs, uu_refs, (dg_ref, du_ref) = refs[0], refs[1:1 + n], refs[1 + n:1 + 2 * n], refs[-2:]
        at = 0
        for u in range(0, n, 2):
            take = counts[u] + counts[u + 1]
            dy = _rows_of(dy_refs[at:at + take])
            at += take
            g2 = lax.dot_general(dy, wd_ref[...], NT, preferred_element_type=F32)
            for k in range(2):
                g = g2[k * rows:(k + 1) * rows]
                gate = ug_refs[u + k][0, 0].astype(F32)
                up = uu_refs[u + k][0, 0].astype(F32)
                sig = jax.nn.sigmoid(gate)
                dg_ref[u + k] = (g * up * sig * (1.0 + gate * (1.0 - sig))).astype(BF16)
                du_ref[u + k] = (g * (gate * sig)).astype(BF16)

    u_specs = [_along((1, 1, rows, step), 3, f'r{r}', h, 0, 0) for _, r, h in units]
    o_spec = _along((n, rows, step), 2, lead, 0, 0)
    out = jax.ShapeDtypeStruct((ug4.shape[0] * ug4.shape[1], rows, width), BF16)
    args = [a for a, _ in pieces] + [wd] + [ug4] * n + [uu4] * n + list(old)
    return _call(
        body, args, place=place, deps=deps, aliases={len(args) - 1: 0, len(args): 1} if old else None,
        flops=2 * n * rows * hidden * width, nbytes=2 * (n * rows * (hidden + 4 * width) + width * hidden),
        grid=(width // step,),
        in_specs=[s for _, s in pieces] + [_along((step, hidden), 0, 0, 0)] + u_specs + u_specs
        + [pl.BlockSpec(memory_space=pl.ANY)] * len(old),
        out_specs=[o_spec, o_spec], out_shape=[out, out])


def _partials(dg3, du3, lead, wg, wu, targets, shapes, deps=(), step=256):
    n, (_, rows, width) = len(targets), dg3.shape
    hidden = wg.shape[0]
    half = hidden // 2

    def body(dg_ref, du_ref, wga_ref, wgb_ref, wua_ref, wub_ref, *outs):
        dg = dg_ref[...].reshape(n * rows, width)
        du = du_ref[...].reshape(n * rows, width)
        wg_t = jnp.concatenate([wga_ref[...], wgb_ref[...]], axis=0)
        wu_t = jnp.concatenate([wua_ref[...], wub_ref[...]], axis=0)
        acc = (lax.dot_general(dg, wg_t, NT, preferred_element_type=F32)
               + lax.dot_general(du, wu_t, NT, preferred_element_type=F32)).astype(BF16)
        for u, pair in enumerate(targets):
            for side, (o, lead) in enumerate(pair):
                outs[o][lead] = acc[u * rows:(u + 1) * rows, side * step:(side + 1) * step]

    tiles = half // step
    left, right = _along((step, width), 0, 0, 0), _along((step, width), 0, 0, 0, offset=tiles)
    return _call(
        body, (dg3, du3, wg, wg, wu, wu), deps=deps,
        flops=4 * n * rows * hidden * width, nbytes=2 * (n * rows * (hidden + 2 * width) + 2 * width * hidden),
        grid=(tiles,),
        in_specs=[_fixed((n, rows, width), lead, 0, 0)] * 2 + [left, right, left, right],
        out_specs=[_along((m, rows, step), 2, 0, 0, 0) for m in shapes],
        out_shape=[jax.ShapeDtypeStruct((m, rows, half), BF16) for m in shapes])


def _wdown(zt, pieces, deps, step=512):
    width, tok = zt.shape
    hidden = pieces[0][0].shape[-1]

    def body(zt_ref, *refs):
        refs[-1][...] = lax.dot_general(zt_ref[...], _rows_of(refs[:-1]), NN, preferred_element_type=F32)

    return _call(
        body, [zt] + [a for a, _ in pieces], deps=deps,
        flops=2 * tok * width * hidden, nbytes=2 * tok * (width + hidden) + 4 * width * hidden,
        grid=(hidden // step,), in_specs=[_fixed(zt.shape, 0, 0)] + [s for _, s in pieces],
        out_specs=_along((width, step), 1, 0, 0),
        out_shape=jax.ShapeDtypeStruct((width, hidden), F32))


def _wcol(d_rows, pieces, deps, step=512):
    tok, width = d_rows.shape
    hidden = pieces[0][0].shape[-1]

    def body(d_ref, *refs):
        xt = _rows_of(refs[:-1]).T
        refs[-1][...] = lax.dot_general(xt, d_ref[...], NN, preferred_element_type=F32)

    return _call(
        body, [d_rows] + [a for a, _ in pieces], deps=deps,
        flops=2 * tok * width * hidden, nbytes=2 * tok * (width + hidden) + 4 * width * hidden,
        grid=(hidden // step,), in_specs=[_fixed(d_rows.shape, 0, 0)] + [s for _, s in pieces],
        out_specs=_along((step, width), 0, 0, 0),
        out_shape=jax.ShapeDtypeStruct((hidden, width), F32))


def _sum(refs):
    total = refs[0][...].astype(F32)
    for r in refs[1:]:
        total = total + r[...].astype(F32)
    return total


def _far_sums(terms_a, terms_b, deps, step=512):
    both, rows, half = terms_a[0].shape
    n = len(terms_a)

    def body(*refs):
        for side, terms in enumerate((refs[:n], refs[n:2 * n])):
            total = _sum(terms)
            for h in range(both):
                refs[2 * n + side * both + h][...] = total[h]

    spec = _along((both, rows, step), 2, 0, 0, 0)
    return _call(
        body, [*terms_a, *terms_b], flops=16 * rows * half, nbytes=48 * rows * half, deps=deps,
        grid=(half // step,), in_specs=[spec] * (2 * n), out_specs=[_along((rows, step), 1, 0, 0)] * (2 * both),
        out_shape=[jax.ShapeDtypeStruct((rows, half), F32)] * (2 * both))


def _final_sums(terms_a, terms_b, far_a, far_b, chunk, whole, deps, step=64):
    rows, half = far_a.shape
    n = len(terms_a)
    steps = rows // step
    old = [] if whole is None else [whole]

    def body(*refs):
        o_ref = refs[-1]
        o_ref[:, :half] = (_sum(refs[:n])[0] + refs[2 * n][...]).astype(BF16)
        o_ref[:, half:] = (_sum(refs[n:2 * n])[0] + refs[2 * n + 1][...]).astype(BF16)

    args = [*terms_a, *terms_b, far_a, far_b] + old
    return _call(
        body, args, flops=8 * rows * half, nbytes=28 * rows * half, deps=deps, grid=(steps,),
        in_specs=[_along((1, step, half), 1, chunk, 0, 0)] * (2 * n)
        + [_along((step, half), 0, 0, 0)] * 2 + [pl.BlockSpec(memory_space=pl.ANY)] * len(old),
        out_specs=_along((step, 2 * half), 0, 0, 0, offset=chunk * steps),
        out_shape=jax.ShapeDtypeStruct((CHUNKS * rows, 2 * half), BF16),
        aliases={len(args) - 1: 0} if old else None)


def solution(mesh):
    group = mesh.shape['tp']

    def send(value, away):
        return lax.ppermute(value, 'tp', [(d, d ^ away) for d in range(group)])


    def layer(x_loc, wg_loc, wu_loc, wd_loc, ug_loc, uu_loc, dy_loc):
        tok, hidden = x_loc.shape
        width = wd_loc.shape[0]
        rows = tok // CHUNKS
        place = lax.axis_index('tp').astype(jnp.int32) ^ jnp.arange(group, dtype=jnp.int32)
        ug4 = ug_loc.reshape(group, CHUNKS, rows, width)
        uu4 = uu_loc.reshape(group, CHUNKS, rows, width)
        hs = range(CHUNKS)

        dy_mate = send(dy_loc, 1)
        halves = [dy_loc[:rows], dy_loc[rows:]]
        dy_x, dy_y = [None, None], [None, None]
        for h in hs:
            dy_x[h] = send(halves[h], 2)
            dy_y[1 - h] = send(halves[1 - h], 4)
        zt = _z_transposed(place, ug4, uu4, 0, 4, None, ())

        def piece(a, h=0):
            return ([(a, _fixed((rows, hidden), h, 0))],)

        units = [piece(a, h) + (r, h) for r, a in ((0, dy_loc), (1, dy_mate)) for h in hs]
        dg, du = _mid_grads(place, units, wd_loc, ug4, uu4, 2, (), (zt,))
        dy_x[0], dy_y[1], dg = lax.optimization_barrier((dy_x[0], dy_y[1], dg))
        dy_d = [send(dy_x[0], 4), send(dy_y[1], 2)]
        keep_a, keep_b, give_a, give_b = _partials(
            dg, du, 2, wg_loc, wu_loc,
            [((0, 0), (1, 0)), ((0, 1), (1, 1)), ((2, 0), (3, 0)), ((2, 1), (3, 1))], [2, 2, 2, 2])
        mate_a, mate_b = send(give_a, 1), send(give_b, 1)
        x_now, keep_a = lax.optimization_barrier((x_loc, keep_a))
        x_x0, x_y0 = send(x_now, 2), send(x_now, 4)
        dy_x[1], dy_y[0], keep_a = lax.optimization_barrier((dy_x[1], dy_y[0], keep_a))
        dy_xm, dy_ym = [send(a, 1) for a in dy_x], [send(a, 1) for a in dy_y]
        zt = _z_transposed(place, ug4, uu4, 4, 4, zt, (keep_a, dy_x[1], dy_y[0]))

        near = ((2, dy_x), (3, dy_xm), (4, dy_y), (5, dy_ym))
        units = [piece(ps[h]) + (r, h) for r, ps in near for h in hs]
        dg, du = _mid_grads(place, units, wd_loc, ug4, uu4, 0, (dg, du), (zt, keep_a))
        dy_d = list(lax.optimization_barrier((*dy_d, dg))[:2])
        dy_dm = [send(a, 1) for a in dy_d]
        sides = ((0, 2), (1, 3), (6, 4), (7, 5))
        targets = [((a, h), (b, h)) for a, b in sides for h in hs]
        p = _partials(dg, du, 0, wg_loc, wu_loc, targets, [2] * 8)
        x_x0, x_y0, near_x, near_y, x_own = lax.optimization_barrier((x_x0, x_y0, p[0], p[4], x_loc))
        x_d = [send(x_x0[:rows], 4), send(x_y0[rows:], 2)]
        x_mate, x_x1, x_y1 = send(x_own, 1), send(x_x0, 1), send(x_y0, 1)
        near_x, near_y = send(near_x, 2), send(near_y, 4)
        pass_a, pass_b = [p[6], send(p[7], 1)], [p[2], send(p[3], 1)]

        units = [piece(a) + (r, h) for r, ps in ((6, dy_d), (7, dy_dm)) for h, a in enumerate(ps)]
        dg, du = _mid_grads(place, units, wd_loc, ug4, uu4, 3, (dg, du), (p[0],))
        targets = [((2 * k, h), (2 * k + 1, h)) for k in range(2) for h in hs]
        q = _partials(dg, du, 3, wg_loc, wu_loc, targets, [2] * 4)
        pass_a += [send(q[0], 2), send(q[2], 3)]
        pass_b += [send(q[1], 4), send(q[3], 5)]

        late_x, late_y, _ = lax.optimization_barrier((p[1], p[5], q[0]))
        done_a = [keep_a, mate_a, near_x, send(late_x, 3)]
        done_b = [keep_b, mate_b, near_y, send(late_y, 5)]

        x_d = list(lax.optimization_barrier((*x_d, q[0]))[:2])
        x_dm = [send(a, 1) for a in x_d]
        strip = 512

        def cols(a):
            return (a, _along((a.shape[0], strip), 1, 0, 0))

        dy_rows = [cols(a) for a in (dy_loc, dy_mate, *dy_x, *dy_xm, *dy_y, *dy_ym, *dy_d, *dy_dm)]
        grad_wd = _wdown(zt, dy_rows, (q[0],), strip)
        x_rows = [cols(a) for a in (x_x0, x_x1, x_y0, x_y1, x_loc, x_mate, *x_d, *x_dm)]
        grad_wg = _wcol(dg.reshape(-1, width), x_rows, (grad_wd,))
        far = _far_sums(pass_a, pass_b, (grad_wg,))
        far_a, far_b = [send(a, 4) for a in far[:2]], [send(a, 2) for a in far[2:]]
        grad_wu = _wcol(du.reshape(-1, width), x_rows, (far[0],))
        grad_x = _final_sums(done_a, done_b, far_a[0], far_b[0], 0, None, (grad_wu,))
        grad_x = _final_sums(done_a, done_b, far_a[1], far_b[1], 1, grad_x, ())
        return grad_x, grad_wg, grad_wu, grad_wd

    row_spec = P(('dp', 'tp'), None)
    col_spec = P(None, 'tp')
    part_cols = P('dp', 'tp')
    return jax.shard_map(layer, mesh=mesh,
                         in_specs=(row_spec, col_spec, col_spec, P('tp', None), part_cols, part_cols, row_spec),
                         out_specs=(row_spec, part_cols, part_cols, row_spec),
                         check_vma=False)
```

profile of v0, /device:TPU:0, one launch (start us, length us, event | category | flops | bytes accessed | tf_op | source)
XLA Modules:
  0.0 719.0 jit_solution(7286472302015361945)
XLA Ops:
  1.5 4.7 fusion
  11.3 10.4 %shard_map.102.refs_14_.refs_3_ = bf16[1792,4096]{1,0:T(8,128)(2,1)} custom-call(s32[8]{0:T(128)} %iota_xor_fusion.refs_0_, bf16[8,2,256,1792]{3,2,1,0:T(8,128)(2,1)} %bitcast.4, bf16[8,2,256,1792]{3,2,1,0:T(8,128)(2,1)} %bitcast.22), custom_call_target="tpu_custom_call" | custom-call | flops 29360128 | bytes 22020096 | tf_op jit(solution)/shard_map/pallas_call | solution.py:23
  21.7 25.8 %shard_map.103 = (bf16[16,256,1792]{2,1,0:T(8,128)(2,1)}, bf16[16,256,1792]{2,1,0:T(8,128)(2,1)}) custom-call(s32[8]{0:T(128)} %iota_xor_fusion.refs_0_, bf16[512,4096]{1,0:T(8,128)(2,1)} %refs_1_.3, bf16[512,4096]{1,0:T(8,128)(2,1)} %refs_1_.3, bf16[512,4096]{1,0:T(8,128)(2,1)} %collective-permute-done.4.refs_3_.refs_4_.refs_2_, ...), custom_call_target="tpu_custom_call" | custom-call | flops 15032385536 | bytes 37748736 | tf_op jit(solution)/shard_map/pallas_call | solution.py:23
  47.4 8.1 %collective-permute-done.2.refs_1_.refs_3_ = bf16[256,4096]{1,0:T(8,128)(2,1)} collective-permute-done((bf16[256,4096]{1,0:T(8,128)(2,1)}, bf16[256,4096]{1,0:T(8,128)(2,1)}, u32[]{:S(2)}, u32[]{:S(2)}) %collective-permute-start.2) | collective-permute-done | bytes 2097184 | tf_op jit(solution)/shard_map/ppermute | solution.py:224
  57.5 37.5 %shard_map.104 = (bf16[2,256,2048]{2,1,0:T(8,128)(2,1)}, bf16[2,256,2048]{2,1,0:T(8,128)(2,1)}, bf16[2,256,2048]{2,1,0:T(8,128)(2,1)}, bf16[2,256,2048]{2,1,0:T(8,128)(2,1)}) custom-call(bf16[16,256,1792]{2,1,0:T(8,128)(2,1)} %get-tuple-element.50.refs_0_.refs_26_, bf16[16,256,1792]{2,1,0:T(8,128)(2,1)} %get-tuple-element.51.refs_1_.refs_27_, ...), custom_call_target="tpu_custom_call" | custom-call | flops 30064771072 | bytes 45088768 | tf_op jit(solution)/shard_map/pallas_call | solution.py:23
  95.0 5.1 collective-permute-done.refs_5_.refs_2_.refs_4_
  104.3 10.4 %shard_map.105.refs_28_.refs_0_ = bf16[1792,4096]{1,0:T(8,128)(2,1)} custom-call(s32[8]{0:T(128)} %iota_xor_fusion.refs_0_, bf16[8,2,256,1792]{3,2,1,0:T(8,128)(2,1)} %bitcast.9, bf16[8,2,256,1792]{3,2,1,0:T(8,128)(2,1)} %bitcast.27, bf16[1792,4096]{1,0:T(8,128)(2,1)} %shard_map.102.refs_14_.refs_3_, ...), custom_call_target="tpu_custom_call", output_to_operand_aliasing={{}: (3, {})} | custom-call | flops 29360128 | bytes 22020096 | tf_op jit(solution)/shard_map/pallas_call | solution.py:23
  117.2 47.0 %shard_map.106 = (bf16[16,256,1792]{2,1,0:T(8,128)(2,1)}, bf16[16,256,1792]{2,1,0:T(8,128)(2,1)}) custom-call(s32[8]{0:T(128)} %iota_xor_fusion.refs_0_, bf16[256,4096]{1,0:T(8,128)(2,1)} %collective-permute-done.2.refs_1_.refs_3_, bf16[256,4096]{1,0:T(8,128)(2,1)} %copy-done, ...), custom_call_target="tpu_custom_call", output_to_operand_aliasing={{0}: (26, {}), {1}: (27, {})} | custom-call | flops 30064771072 | bytes 60817408 | tf_op jit(solution)/shard_map/pallas_call | solution.py:23
  164.7 71.1 %shard_map.107 = (bf16[2,256,2048]{2,1,0:T(8,128)(2,1)}, bf16[2,256,2048]{2,1,0:T(8,128)(2,1)}, bf16[2,256,2048]{2,1,0:T(8,128)(2,1)}, bf16[2,256,2048]{2,1,0:T(...) custom-call(bf16[16,256,1792]{2,1,0:T(8,128)(2,1)} %get-tuple-elemen, ...), custom_call_target="tpu_custom_call" | custom-call | flops 60129542144 | bytes 60817408 | tf_op jit(solution)/shard_map/pallas_call | solution.py:23
  235.9 16.2 %collective-permute-done.6.refs_1_ = bf16[512,4096]{1,0:T(8,128)(2,1)} collective-permute-done((bf16[512,4096]{1,0:T(8,128)(2,1)}, bf16[512,4096]{1,0:T(8,128)(2,1)}, u32[]{:S(2)}, u32[]{:S(2)}) %collective-permute-start.6) | collective-permute-done | bytes 4194336 | tf_op jit(solution)/shard_map/ppermute | solution.py:224
  252.1 3.2 slice.14
  260.3 25.8 %shard_map.108 = (bf16[16,256,1792]{2,1,0:T(8,128)(2,1)}, bf16[16,256,1792]{2,1,0:T(8,128)(2,1)}) custom-call(s32[8]{0:T(128)} %iota_xor_fusion.refs_0_, bf16[256,4096]{1,0:T(8,128)(2,1)} %collective-permute-done.13.refs_1_.refs_11_, bf16[256,4096]{1,0:T(8,128)(2,1)} %collective-permute-done.14.refs_2_.refs_12_, ...), custom_call_target="tpu_custom_call", output_to_operand_aliasing={{0}: (14, {}), {1}: (15, {})} | custom-call | flops 15032385536 | bytes 37748736 | tf_op jit(solution)/shard_map/pallas_call | solution.py:23
  286.0 37.6 %shard_map.109 = (bf16[2,256,2048]{2,1,0:T(8,128)(2,1)}, bf16[2,256,2048]{2,1,0:T(8,128)(2,1)}, bf16[2,256,2048]{2,1,0:T(8,128)(2,1)}, bf16[2,256,2048]{2,1,0:T(8,128)(2,1)}) custom-call(bf16[16,256,1792]{2,1,0:T(8,128)(2,1)} %get-tuple-element.70.refs_0_, bf16[16,256,1792]{2,1,0:T(8,128)(2,1)} %get-tuple-element.71.refs_1_, bf16[4096,1792]{1,0:T(8,128)(2,1)} %refs_3_.5, ...), custom_call_target="tpu_custom_call" | custom-call | flops 30064771072 | bytes 45088768 | tf_op jit(solution)/shard_map/pallas_call | solution.py:23
  327.3 45.1 %collective-permute-done.22.refs_2_ = bf16[2,256,2048]{2,1,0:T(8,128)(2,1)} collective-permute-done((bf16[2,256,2048]{2,1,0:T(8,128)(2,1)}, bf16[2,256,2048]{2,1,0:T(8,128)(2,1)}, u32[]{:S(2)}, u32[]{:S(2)}) %collective-permute-start.22) | collective-permute-done | bytes 2097184 | tf_op jit(solution)/shard_map/ppermute | solution.py:224
  372.4 43.5 %collective-permute-done.23.refs_3_ = bf16[2,256,2048]{2,1,0:T(8,128)(2,1)} collective-permute-done((bf16[2,256,2048]{2,1,0:T(8,128)(2,1)}, bf16[2,256,2048]{2,1,0:T(8,128)(2,1)}, u32[]{:S(2)}, u32[]{:S(2)}) %collective-permute-start.23) | collective-permute-done | bytes 2097184 | tf_op jit(solution)/shard_map/ppermute | solution.py:224
  418.4 71.2 %shard_map.110.refs_11_ = f32[1792,4096]{1,0:T(8,128)} custom-call(bf16[1792,4096]{1,0:T(8,128)(2,1)} %shard_map.105.refs_28_.refs_0_, bf16[512,4096]{1,0:T(8,128)(2,1)} %refs_1_.3, bf16[512,4096]{1,0:T(8,128)(2,1)} %collective-permute-done.4.refs_3_.refs_4_.refs_2_, bf16[256,4096]{1,0:T(8,128)(2,1)} %collective-permute-done.2.refs_1_.refs_3_, ...), custom_call_target="tpu_custom_call" | custom-call | flops 60129542144 | bytes 77594624 | tf_op jit(solution)/shard_map/pallas_call | solution.py:23
  493.4 71.5 %shard_map.111.refs_8_ = f32[4096,1792]{1,0:T(8,128)} custom-call(bf16[4096,1792]{1,0:T(8,128)(2,1)} %bitcast.40, bf16[512,4096]{1,0:T(8,128)(2,1)} %collective-permute-done.6.refs_1_, bf16[512,4096]{1,0:T(8,128)(2,1)} %collective-permute-done.27.refs_2_, bf16[512,4096]{1,0:T(8,128)(2,1)} %collective-permute-done.7.refs_3_, ...), custom_call_target="tpu_custom_call" | custom-call | flops 60129542144 | bytes 77594624 | tf_op jit(solution)/shard_map/pallas_call | solution.py:23
  564.9 9.5 %shard_map.112 = (f32[256,2048]{1,0:T(8,128)}, f32[256,2048]{1,0:T(8,128)}, f32[256,2048]{1,0:T(8,128)}, f32[256,2048]{1,0:T(8,128)}) custom-call(bf16[2,256,2048]{2,1,0:T(8,128)(2,1)} %get-tuple-element.78.refs_0_, bf16[2,256,2048]{2,1,0:T(8,128)(2,1)} %collective-permute-done.21.refs_1_, bf16[2,256,2048]{2,1,0:T(8,128)(2,1)} %collective-permute-done.22.refs_2_, ...), custom_call_target="tpu_custom_call" | custom-call | flops 8388608 | bytes 25165824 | tf_op jit(solution)/shard_map/pallas_call | solution.py:23
  577.8 5.9 collective-permute-done.12.refs_2_
  584.7 71.7 %shard_map.113.refs_10_ = f32[4096,1792]{1,0:T(8,128)} custom-call(bf16[4096,1792]{1,0:T(8,128)(2,1)} %bitcast.41, bf16[512,4096]{1,0:T(8,128)(2,1)} %collective-permute-done.6.refs_1_, bf16[512,4096]{1,0:T(8,128)(2,1)} %collective-permute-done.27.refs_2_, bf16[512,4096]{1,0:T(8,128)(2,1)} %collective-permute-done.7.refs_3_, ...), custom_call_target="tpu_custom_call" | custom-call | flops 60129542144 | bytes 77594624 | tf_op jit(solution)/shard_map/pallas_call | solution.py:23
  656.3 11.9 %collective-permute-done.36.refs_8_ = f32[256,2048]{1,0:T(8,128)} collective-permute-done((f32[256,2048]{1,0:T(8,128)}, f32[256,2048]{1,0:T(8,128)}, u32[]{:S(2)}, u32[]{:S(2)}) %collective-permute-start.36) | collective-permute-done | bytes 2097184 | tf_op jit(solution)/shard_map/ppermute | solution.py:224
  668.2 6.5 shard_map.114.refs_10_
  674.8 37.4 %collective-permute-done.34.refs_8_ = f32[256,2048]{1,0:T(8,128)} collective-permute-done((f32[256,2048]{1,0:T(8,128)}, f32[256,2048]{1,0:T(8,128)}, u32[]{:S(2)}, u32[]{:S(2)}) %collective-permute-start.34) | collective-permute-done | bytes 2097184 | tf_op jit(solution)/shard_map/ppermute | solution.py:224
  712.2 6.5 shard_map.115
  (76 shorter events, 34.5 us)
Async XLA Ops:
  10.2 89.9 %collective-permute-start = (bf16[256,4096]{1,0:T(8,128)(2,1)}, bf16[256,4096]{1,0:T(8,128)(2,1)S(1)}, u32[]{:S(2)}, u32[]{:S(2)}) collective-permute-start(bf16[256,4096]{1,0:T(8,128)(2,1)} %get-tuple-element.95), channel_id=1, source_target_pairs={{0,2},{1,3},{2,0},{3,1},{4,6},{5,7},{6,4},{7,5}} | collective-permute-start | bytes 6291464 | tf_op jit(solution)/shard_map/ppermute | solution.py:224
  10.8 90.9 %collective-permute-start.1 = (bf16[256,4096]{1,0:T(8,128)(2,1)}, bf16[256,4096]{1,0:T(8,128)(2,1)}, u32[]{:S(2)}, u32[]{:S(2)}) collective-permute-start(bf16[256,4096]{1,0:T(8,128)(2,1)} %get-tuple-element.94), channel_id=1, source_target_pairs={{0,4},{1,5},{2,6},{3,7},{4,0},{5,1},{6,2},{7,3}} | collective-permute-start | bytes 6291464 | tf_op jit(solution)/shard_map/ppermute | solution.py:224
  115.2 136.9 %collective-permute-start.6 = (bf16[512,4096]{1,0:T(8,128)(2,1)}, bf16[512,4096]{1,0:T(8,128)(2,1)}, u32[]{:S(2)}, u32[]{:S(2)}) collective-permute-start(bf16[512,4096]{1,0:T(8,128)(2,1)} %refs_5_.13), channel_id=1, source_target_pairs={{0,2},{1,3},{2,0},{3,1},{4,6},{5,7},{6,4},{7,5}} | collective-permute-start | bytes 12582920 | tf_op jit(solution)/shard_map/ppermute | solution.py:224
  116.7 135.4 %collective-permute-start.7 = (bf16[512,4096]{1,0:T(8,128)(2,1)}, bf16[512,4096]{1,0:T(8,128)(2,1)}, u32[]{:S(2)}, u32[]{:S(2)}) collective-permute-start(bf16[512,4096]{1,0:T(8,128)(2,1)} %refs_5_.13), channel_id=1, source_target_pairs={{0,4},{1,5},{2,6},{3,7},{4,0},{5,1},{6,2},{7,3}} | collective-permute-start | bytes 12582920 | tf_op jit(solution)/shard_map/ppermute | solution.py:224
  164.2 94.7 %collective-permute-start.15 = (bf16[256,4096]{1,0:T(8,128)(2,1)}, bf16[256,4096]{1,0:T(8,128)(2,1)S(1)}, u32[]{:S(2)}, u32[]{:S(2)}) collective-permute-start(bf16[256,4096]{1,0:T(8,128)(2,1)} %collective-permute-done.13.refs_1_.refs_11_), channel_id=1, source_target_pairs={{0,1},{1,0},{2,3},{3,2},{4,5},{5,4},{6,7},{7,6}} | collective-permute-start | bytes 6291464 | tf_op jit(solution)/shard_map/ppermute | solution.py:224
  164.2 95.0 %collective-permute-start.16 = (bf16[256,4096]{1,0:T(8,128)(2,1)}, bf16[256,4096]{1,0:T(8,128)(2,1)}, u32[]{:S(2)}, u32[]{:S(2)}) collective-permute-start(bf16[256,4096]{1,0:T(8,128)(2,1)} %collective-permute-done.14.refs_2_.refs_12_), channel_id=1, source_target_pairs={{0,1},{1,0},{2,3},{3,2},{4,5},{5,4},{6,7},{7,6}} | collective-permute-start | bytes 6291464 | tf_op jit(solution)/shard_map/ppermute | solution.py:224
  235.8 88.5 %collective-permute-start.21 = (bf16[2,256,2048]{2,1,0:T(8,128)(2,1)}, bf16[2,256,2048]{2,1,0:T(8,128)(2,1)}, u32[]{:S(2)}, u32[]{:S(2)}) collective-permute-start(bf16[2,256,2048]{2,1,0:T(8,128)(2,1)} %get-tuple-element.79), channel_id=1, source_target_pairs={{0,1},{1,0},{2,3},{3,2},{4,5},{5,4},{6,7},{7,6}} | collective-permute-start | bytes 6291464 | tf_op jit(solution)/shard_map/ppermute | solution.py:224
  252.1 75.0 %collective-permute-start.24 = (bf16[2,256,2048]{2,1,0:T(8,128)(2,1)}, bf16[2,256,2048]{2,1,0:T(8,128)(2,1)}, u32[]{:S(2)}, u32[]{:S(2)}) collective-permute-start(bf16[2,256,2048]{2,1,0:T(8,128)(2,1)} %get-tuple-element.82), channel_id=1, source_target_pairs={{0,1},{1,0},{2,3},{3,2},{4,5},{5,4},{6,7},{7,6}} | collective-permute-start | bytes 6291464 | tf_op jit(solution)/shard_map/ppermute | solution.py:224
  324.3 91.6 %collective-permute-start.23 = (bf16[2,256,2048]{2,1,0:T(8,128)(2,1)}, bf16[2,256,2048]{2,1,0:T(8,128)(2,1)}, u32[]{:S(2)}, u32[]{:S(2)}) collective-permute-start(bf16[2,256,2048]{2,1,0:T(8,128)(2,1)} %get-tuple-element.80), channel_id=1, source_target_pairs={{0,3},{1,2},{2,1},{3,0},{4,7},{5,6},{6,5},{7,4}} | collective-permute-start | bytes 6291464 | tf_op jit(solution)/shard_map/ppermute | solution.py:224
  325.2 91.6 %collective-permute-start.25 = (bf16[2,256,2048]{2,1,0:T(8,128)(2,1)}, bf16[2,256,2048]{2,1,0:T(8,128)(2,1)}, u32[]{:S(2)}, u32[]{:S(2)}) collective-permute-start(bf16[2,256,2048]{2,1,0:T(8,128)(2,1)} %get-tuple-element.83), channel_id=1, source_target_pairs={{0,4},{1,5},{2,6},{3,7},{4,0},{5,1},{6,2},{7,3}} | collective-permute-start | bytes 6291464 | tf_op jit(solution)/shard_map/ppermute | solution.py:224
  326.7 91.4 %collective-permute-start.26 = (bf16[2,256,2048]{2,1,0:T(8,128)(2,1)}, bf16[2,256,2048]{2,1,0:T(8,128)(2,1)}, u32[]{:S(2)}, u32[]{:S(2)}) collective-permute-start(bf16[2,256,2048]{2,1,0:T(8,128)(2,1)} %get-tuple-element.84), channel_id=1, source_target_pairs={{0,5},{1,4},{2,7},{3,6},{4,1},{5,0},{6,3},{7,2}} | collective-permute-start | bytes 6291464 | tf_op jit(solution)/shard_map/ppermute | solution.py:224
  327.1 162.4 %collective-permute-start.27 = (bf16[512,4096]{1,0:T(8,128)(2,1)}, bf16[512,4096]{1,0:T(8,128)(2,1)}, u32[]{:S(2)}, u32[]{:S(2)}) collective-permute-start(bf16[512,4096]{1,0:T(8,128)(2,1)} %collective-permute-done.6.refs_1_), channel_id=1, source_target_pairs={{0,1},{1,0},{2,3},{3,2},{4,5},{5,4},{6,7},{7,6}} | collective-permute-start | bytes 12582920 | tf_op jit(solution)/shard_map/ppermute | solution.py:224
  372.4 117.4 %collective-permute-start.28 = (bf16[512,4096]{1,0:T(8,128)(2,1)}, bf16[512,4096]{1,0:T(8,128)(2,1)}, u32[]{:S(2)}, u32[]{:S(2)}) collective-permute-start(bf16[512,4096]{1,0:T(8,128)(2,1)} %collective-permute-done.7.refs_3_), channel_id=1, source_target_pairs={{0,1},{1,0},{2,3},{3,2},{4,5},{5,4},{6,7},{7,6}} | collective-permute-start | bytes 12582920 | tf_op jit(solution)/shard_map/ppermute | solution.py:224
  415.9 74.2 %collective-permute-start.29 = (bf16[512,4096]{1,0:T(8,128)(2,1)}, bf16[512,4096]{1,0:T(8,128)(2,1)}, u32[]{:S(2)}, u32[]{:S(2)}) collective-permute-start(bf16[512,4096]{1,0:T(8,128)(2,1)} %refs_5_.13), channel_id=1, source_target_pairs={{0,1},{1,0},{2,3},{3,2},{4,5},{5,4},{6,7},{7,6}} | collective-permute-start | bytes 12582920 | tf_op jit(solution)/shard_map/ppermute | solution.py:224
  489.6 84.9 %collective-permute-start.18 = (bf16[2,256,2048]{2,1,0:T(8,128)(2,1)}, bf16[2,256,2048]{2,1,0:T(8,128)(2,1)S(1)}, u32[]{:S(2)}, u32[]{:S(2)}) collective-permute-start(bf16[2,256,2048]{2,1,0:T(8,128)(2,1)} %get-tuple-element.75), channel_id=1, source_target_pairs={{0,1},{1,0},{2,3},{3,2},{4,5},{5,4},{6,7},{7,6}} | collective-permute-start | bytes 6291464 | tf_op jit(solution)/shard_map/ppermute | solution.py:224
  489.9 85.1 %collective-permute-start.5 = (bf16[2,256,2048]{2,1,0:T(8,128)(2,1)}, bf16[2,256,2048]{2,1,0:T(8,128)(2,1)}, u32[]{:S(2)}, u32[]{:S(2)}) collective-permute-start(bf16[2,256,2048]{2,1,0:T(8,128)(2,1)} %get-tuple-element.55), channel_id=1, source_target_pairs={{0,1},{1,0},{2,3},{3,2},{4,5},{5,4},{6,7},{7,6}} | collective-permute-start | bytes 6291464 | tf_op jit(solution)/shard_map/ppermute | solution.py:224
  490.1 86.4 %collective-permute-start.17 = (bf16[2,256,2048]{2,1,0:T(8,128)(2,1)}, bf16[2,256,2048]{2,1,0:T(8,128)(2,1)}, u32[]{:S(2)}, u32[]{:S(2)}) collective-permute-start(bf16[2,256,2048]{2,1,0:T(8,128)(2,1)} %get-tuple-element.73), channel_id=1, source_target_pairs={{0,3},{1,2},{2,1},{3,0},{4,7},{5,6},{6,5},{7,4}} | collective-permute-start | bytes 6291464 | tf_op jit(solution)/shard_map/ppermute | solution.py:224
  490.9 86.4 %collective-permute-start.20 = (bf16[2,256,2048]{2,1,0:T(8,128)(2,1)}, bf16[2,256,2048]{2,1,0:T(8,128)(2,1)}, u32[]{:S(2)}, u32[]{:S(2)}) collective-permute-start(bf16[2,256,2048]{2,1,0:T(8,128)(2,1)} %get-tuple-element.77), channel_id=1, source_target_pairs={{0,5},{1,4},{2,7},{3,6},{4,1},{5,0},{6,3},{7,2}} | collective-permute-start | bytes 6291464 | tf_op jit(solution)/shard_map/ppermute | solution.py:224
  492.1 91.6 %collective-permute-start.12 = (bf16[2,256,2048]{2,1,0:T(8,128)(2,1)}, bf16[2,256,2048]{2,1,0:T(8,128)(2,1)}, u32[]{:S(2)}, u32[]{:S(2)}) collective-permute-start(bf16[2,256,2048]{2,1,0:T(8,128)(2,1)} %get-tuple-element.65.refs_16_), channel_id=1, source_target_pairs={{0,2},{1,3},{2,0},{3,1},{4,6},{5,7},{6,4},{7,5}} | collective-permute-start | bytes 6291464 | tf_op jit(solution)/shard_map/ppermute | solution.py:224
  574.4 81.9 %collective-permute-start.19 = (bf16[2,256,2048]{2,1,0:T(8,128)(2,1)}, bf16[2,256,2048]{2,1,0:T(8,128)(2,1)}, u32[]{:S(2)}, u32[]{:S(2)}) collective-permute-start(bf16[2,256,2048]{2,1,0:T(8,128)(2,1)} %get-tuple-element.76), channel_id=1, source_target_pairs={{0,4},{1,5},{2,6},{3,7},{4,0},{5,1},{6,2},{7,3}} | collective-permute-start | bytes 6291464 | tf_op jit(solution)/shard_map/ppermute | solution.py:224
  575.0 93.2 %collective-permute-start.36 = (f32[256,2048]{1,0:T(8,128)}, f32[256,2048]{1,0:T(8,128)}, u32[]{:S(2)}, u32[]{:S(2)}) collective-permute-start(f32[256,2048]{1,0:T(8,128)} %get-tuple-element.92.refs_11_), channel_id=1, source_target_pairs={{0,4},{1,5},{2,6},{3,7},{4,0},{5,1},{6,2},{7,3}} | collective-permute-start | bytes 6291464 | tf_op jit(solution)/shard_map/ppermute | solution.py:224
  576.5 91.7 %collective-permute-start.37 = (f32[256,2048]{1,0:T(8,128)}, f32[256,2048]{1,0:T(8,128)}, u32[]{:S(2)}, u32[]{:S(2)}) collective-permute-start(f32[256,2048]{1,0:T(8,128)} %get-tuple-element.93), channel_id=1, source_target_pairs={{0,2},{1,3},{2,0},{3,1},{4,6},{5,7},{6,4},{7,5}} | collective-permute-start | bytes 6291464 | tf_op jit(solution)/shard_map/ppermute | solution.py:224
  577.3 134.9 %collective-permute-start.34 = (f32[256,2048]{1,0:T(8,128)}, f32[256,2048]{1,0:T(8,128)}, u32[]{:S(2)}, u32[]{:S(2)}) collective-permute-start(f32[256,2048]{1,0:T(8,128)} %get-tuple-element.90), channel_id=1, source_target_pairs={{0,4},{1,5},{2,6},{3,7},{4,0},{5,1},{6,2},{7,3}} | collective-permute-start | bytes 6291464 | tf_op jit(solution)/shard_map/ppermute | solution.py:224
  583.7 128.5 %collective-permute-start.35 = (f32[256,2048]{1,0:T(8,128)}, f32[256,2048]{1,0:T(8,128)}, u32[]{:S(2)}, u32[]{:S(2)}) collective-permute-start(f32[256,2048]{1,0:T(8,128)} %get-tuple-element.91), channel_id=1, source_target_pairs={{0,2},{1,3},{2,0},{3,1},{4,6},{5,7},{6,4},{7,5}} | collective-permute-start | bytes 6291464 | tf_op jit(solution)/shard_map/ppermute | solution.py:224
  (17 other events, 707.9 us)
where the time goes:
time: 727 us; the launch traced here: 719 us
  Pallas kernels  502 us (69%)
  waiting for transfers between devices  178 us (24%)
  starting transfers between devices  24.8 us (3%)
  local copies, waits for them, and re-layouts  12.1 us (2%)
    pallas_call x14, Pallas kernels, _call(): pl.pallas_call(kernel, grid_spec=pltpu.PrefetchScalarGridSpec(num_scalar_...  502 us
    ppermute x38, waiting for transfers between devices, send(): return lax.ppermute(value, 'tp', [(d, d ^ away) for d in range(group)])  178 us
    ppermute x38, starting transfers between devices, send(): return lax.ppermute(value, 'tp', [(d, d ^ away) for d in range(group)])  24.8 us
  transfers between devices with their start and end apart: 38, of which 11 were waited for; matrix products, arithmetic and copies ran while one was open for 2% of the time, Pallas kernels for 69%

commit v1 on v0

--- a/solution.py
+++ b/solution.py
@@ -179,21 +179,18 @@
     return total
 
 
-def _far_sums(terms_a, terms_b, deps, step=512):
-    both, rows, half = terms_a[0].shape
+def _far_sums(terms_a, terms_b, chunk, deps, step=512):
+    _, rows, half = terms_a[0].shape
     n = len(terms_a)
 
     def body(*refs):
-        for side, terms in enumerate((refs[:n], refs[n:2 * n])):
-            total = _sum(terms)
-            for h in range(both):
-                refs[2 * n + side * both + h][...] = total[h]
-
-    spec = _along((both, rows, step), 2, 0, 0, 0)
-    return _call(
-        body, [*terms_a, *terms_b], flops=16 * rows * half, nbytes=48 * rows * half, deps=deps,
-        grid=(half // step,), in_specs=[spec] * (2 * n), out_specs=[_along((rows, step), 1, 0, 0)] * (2 * both),
-        out_shape=[jax.ShapeDtypeStruct((rows, half), F32)] * (2 * both))
+        refs[2 * n][...] = _sum(refs[:n])[0]
+        refs[2 * n + 1][...] = _sum(refs[n:2 * n])[0]
+
+    return _call(
+        body, [*terms_a, *terms_b], flops=8 * rows * half, nbytes=24 * rows * half, deps=deps,
+        grid=(half // step,), in_specs=[_along((1, rows, step), 2, chunk, 0, 0)] * (2 * n),
+        out_specs=[_along((rows, step), 1, 0, 0)] * 2, out_shape=[jax.ShapeDtypeStruct((rows, half), F32)] * 2)
 
 
 def _final_sums(terms_a, terms_b, far_a, far_b, chunk, whole, deps, step=64):
@@ -246,14 +243,16 @@
 
         units = [piece(a, h) + (r, h) for r, a in ((0, dy_loc), (1, dy_mate)) for h in hs]
         dg, du = _mid_grads(place, units, wd_loc, ug4, uu4, 2, (), (zt,))
-        dy_x[0], dy_y[1], dg = lax.optimization_barrier((dy_x[0], dy_y[1], dg))
+        x_own, dg = lax.optimization_barrier((x_loc, dg))
+        x_half = [x_own[:rows], x_own[rows:]]
+        dy_x[0], dy_y[1], dg, *x_half = lax.optimization_barrier((dy_x[0], dy_y[1], dg, *x_half))
         dy_d = [send(dy_x[0], 4), send(dy_y[1], 2)]
         keep_a, keep_b, give_a, give_b = _partials(
             dg, du, 2, wg_loc, wu_loc,
             [((0, 0), (1, 0)), ((0, 1), (1, 1)), ((2, 0), (3, 0)), ((2, 1), (3, 1))], [2, 2, 2, 2])
         mate_a, mate_b = send(give_a, 1), send(give_b, 1)
-        x_now, keep_a = lax.optimization_barrier((x_loc, keep_a))
-        x_x0, x_y0 = send(x_now, 2), send(x_now, 4)
+        *x_half, keep_a = lax.optimization_barrier((*x_half, keep_a))
+        x_x, x_y = [send(a, 2) for a in x_half], [send(a, 4) for a in x_half]
         dy_x[1], dy_y[0], keep_a = lax.optimization_barrier((dy_x[1], dy_y[0], keep_a))
         dy_xm, dy_ym = [send(a, 1) for a in dy_x], [send(a, 1) for a in dy_y]
         zt = _z_transposed(place, ug4, uu4, 4, 4, zt, (keep_a, dy_x[1], dy_y[0]))
@@ -266,9 +265,10 @@
         sides = ((0, 2), (1, 3), (6, 4), (7, 5))
         targets = [((a, h), (b, h)) for a, b in sides for h in hs]
         p = _partials(dg, du, 0, wg_loc, wu_loc, targets, [2] * 8)
-        x_x0, x_y0, near_x, near_y, x_own = lax.optimization_barrier((x_x0, x_y0, p[0], p[4], x_loc))
-        x_d = [send(x_x0[:rows], 4), send(x_y0[rows:], 2)]
-        x_mate, x_x1, x_y1 = send(x_own, 1), send(x_x0, 1), send(x_y0, 1)
+        *xs, near_x, near_y, x_own = lax.optimization_barrier((*x_x, *x_y, p[0], p[4], x_own))
+        x_x, x_y = xs[:2], xs[2:]
+        x_d = [send(x_x[0], 4), send(x_y[1], 2)]
+        x_mate, *xm = [send(a, 1) for a in (x_own, *x_x, *x_y)]
         near_x, near_y = send(near_x, 2), send(near_y, 4)
         pass_a, pass_b = [p[6], send(p[7], 1)], [p[2], send(p[3], 1)]
 
@@ -292,11 +292,15 @@
 
         dy_rows = [cols(a) for a in (dy_loc, dy_mate, *dy_x, *dy_xm, *dy_y, *dy_ym, *dy_d, *dy_dm)]
         grad_wd = _wdown(zt, dy_rows, (q[0],), strip)
-        x_rows = [cols(a) for a in (x_x0, x_x1, x_y0, x_y1, x_loc, x_mate, *x_d, *x_dm)]
+        x_rows = [cols(a) for a in (*x_x, *xm[:2], *x_y, *xm[2:], x_loc, x_mate, *x_d, *x_dm)]
         grad_wg = _wcol(dg.reshape(-1, width), x_rows, (grad_wd,))
-        far = _far_sums(pass_a, pass_b, (grad_wg,))
-        far_a, far_b = [send(a, 4) for a in far[:2]], [send(a, 2) for a in far[2:]]
-        grad_wu = _wcol(du.reshape(-1, width), x_rows, (far[0],))
+        far_a, far_b, last = [], [], (grad_wg,)
+        for h in hs:
+            away_a, away_b = _far_sums(pass_a, pass_b, h, last)
+            far_a.append(send(away_a, 4))
+            far_b.append(send(away_b, 2))
+            last = (away_a,)
+        grad_wu = _wcol(du.reshape(-1, width), x_rows, last)
         grad_x = _final_sums(done_a, done_b, far_a[0], far_b[0], 0, None, (grad_wu,))
         grad_x = _final_sums(done_a, done_b, far_a[1], far_b[1], 1, grad_x, ())
         return grad_x, grad_wg, grad_wu, grad_wd

time: 727 us -> 727 us (level)
    ppermute x38 -> x42, starting transfers between devices: 24.8 us -> 26.7 us  [send(): return lax.ppermute(value, 'tp', [(d, d ^ away) for d in range(group)])]
    pallas_call x14 -> x15, Pallas kernels: 502 us -> 504 us  [_call(): pl.pallas_call(kernel, grid_spec=pltpu.PrefetchScalarGridSpec(num_scalar_...]
    ppermute x38 -> x42, waiting for transfers between devices: 178 us -> 177 us  [send(): return lax.ppermute(value, 'tp', [(d, d ^ away) for d in range(group)])]
  transfers between devices with their start and end apart: 38 -> 42, of which waited for: 11 -> 11; matrix products, arithmetic and copies ran while one was open for 2% -> 1% of each run, Pallas kernels for 69% -> 69%
where the time goes in v1:
time: 727 us; the launch traced here: 719 us
  Pallas kernels  504 us (69%)
  waiting for transfers between devices  177 us (24%)
  starting transfers between devices  26.7 us (4%)
  local copies, waits for them, and re-layouts  9.42 us (1%)
    pallas_call x15, Pallas kernels, _call(): pl.pallas_call(kernel, grid_spec=pltpu.PrefetchScalarGridSpec(num_scalar_...  504 us
    ppermute x42, waiting for transfers between devices, send(): return lax.ppermute(value, 'tp', [(d, d ^ away) for d in range(group)])  177 us
    ppermute x42, starting transfers between devices, send(): return lax.ppermute(value, 'tp', [(d, d ^ away) for d in range(group)])  26.7 us
  transfers between devices with their start and end apart: 42, of which 11 were waited for; matrix products, arithmetic and copies ran while one was open for 1% of the time, Pallas kernels for 69%

profile of v1, /device:TPU:0, one launch (start us, length us, event | category | flops | bytes accessed | tf_op | source)
XLA Modules:
  0.0 718.6 jit_solution(6876911638643838156)
XLA Ops:
  1.5 4.7 fusion.1
  11.3 10.4 %shard_map.102.refs_14_.refs_3_ = bf16[1792,4096]{1,0:T(8,128)(2,1)} custom-call(s32[8]{0:T(128)} %iota_xor_fusion.refs_0_, bf16[8,2,256,1792]{3,2,1,0:T(8,128)(2,1)} %bitcast.4, bf16[8,2,256,1792]{3,2,1,0:T(8,128)(2,1)} %bitcast.22), custom_call_target="tpu_custom_call" | custom-call | flops 29360128 | bytes 22020096 | tf_op jit(solution)/shard_map/pallas_call | solution.py:23
  21.7 25.8 %shard_map.103 = (bf16[16,256,1792]{2,1,0:T(8,128)(2,1)}, bf16[16,256,1792]{2,1,0:T(8,128)(2,1)}) custom-call(s32[8]{0:T(128)} %iota_xor_fusion.refs_0_, bf16[512,4096]{1,0:T(8,128)(2,1)} %refs_1_.3, bf16[512,4096]{1,0:T(8,128)(2,1)} %refs_1_.3, bf16[512,4096]{1,0:T(8,128)(2,1)} %collective-permute-done.4.refs_3_.refs_4_.refs_2_, ...), custom_call_target="tpu_custom_call" | custom-call | flops 15032385536 | bytes 37748736 | tf_op jit(solution)/shard_map/pallas_call | solution.py:23
  47.4 4.7 fusion
  52.1 49.6 %collective-permute-done.2.refs_1_.refs_3_ = bf16[256,4096]{1,0:T(8,128)(2,1)} collective-permute-done((bf16[256,4096]{1,0:T(8,128)(2,1)}, bf16[256,4096]{1,0:T(8,128)(2,1)}, u32[]{:S(2)}, u32[]{:S(2)}) %collective-permute-start.2) | collective-permute-done | bytes 2097184 | tf_op jit(solution)/shard_map/ppermute | solution.py:221
  101.7 37.6 %shard_map.104 = (bf16[2,256,2048]{2,1,0:T(8,128)(2,1)}, bf16[2,256,2048]{2,1,0:T(8,128)(2,1)}, bf16[2,256,2048]{2,1,0:T(8,128)(2,1)}, bf16[2,256,2048]{2,1,0:T(8,128)(2,1)}) custom-call(bf16[16,256,1792]{2,1,0:T(8,128)(2,1)} %get-tuple-element.61.refs_0_.refs_26_, bf16[16,256,1792]{2,1,0:T(8,128)(2,1)} %get-tuple-element.62.refs_1_.refs_27_, ...), custom_call_target="tpu_custom_call" | custom-call | flops 30064771072 | bytes 45088768 | tf_op jit(solution)/shard_map/pallas_call | solution.py:23
  140.7 10.4 %shard_map.105.refs_28_.refs_0_ = bf16[1792,4096]{1,0:T(8,128)(2,1)} custom-call(s32[8]{0:T(128)} %iota_xor_fusion.refs_0_, bf16[8,2,256,1792]{3,2,1,0:T(8,128)(2,1)} %bitcast.9, bf16[8,2,256,1792]{3,2,1,0:T(8,128)(2,1)} %bitcast.27, bf16[1792,4096]{1,0:T(8,128)(2,1)} %shard_map.102.refs_14_.refs_3_, ...), custom_call_target="tpu_custom_call", output_to_operand_aliasing={{}: (3, {})} | custom-call | flops 29360128 | bytes 22020096 | tf_op jit(solution)/shard_map/pallas_call | solution.py:23
  156.3 47.0 %shard_map.106 = (bf16[16,256,1792]{2,1,0:T(8,128)(2,1)}, bf16[16,256,1792]{2,1,0:T(8,128)(2,1)}) custom-call(s32[8]{0:T(128)} %iota_xor_fusion.refs_0_, bf16[256,4096]{1,0:T(8,128)(2,1)} %collective-permute-done.2.refs_1_.refs_3_, bf16[256,4096]{1,0:T(8,128)(2,1)} %copy-done, ...), custom_call_target="tpu_custom_call", output_to_operand_aliasing={{0}: (26, {}), {1}: (27, {})} | custom-call | flops 30064771072 | bytes 60817408 | tf_op jit(solution)/shard_map/pallas_call | solution.py:23
  203.9 40.9 %collective-permute-done.6.refs_1_ = bf16[256,4096]{1,0:T(8,128)(2,1)} collective-permute-done((bf16[256,4096]{1,0:T(8,128)(2,1)}, bf16[256,4096]{1,0:T(8,128)(2,1)}, u32[]{:S(2)}, u32[]{:S(2)}) %collective-permute-start.6) | collective-permute-done | bytes 2097184 | tf_op jit(solution)/shard_map/ppermute | solution.py:221
  244.8 71.1 %shard_map.107 = (bf16[2,256,2048]{2,1,0:T(8,128)(2,1)}, bf16[2,256,2048]{2,1,0:T(8,128)(2,1)}, bf16[2,256,2048]{2,1,0:T(8,128)(2,1)}, bf16[2,256,2048]{2,1,0:T(...) custom-call(bf16[16,256,1792]{2,1,0:T(8,128)(2,1)} %get-tuple-elemen, ...), custom_call_target="tpu_custom_call" | custom-call | flops 60129542144 | bytes 60817408 | tf_op jit(solution)/shard_map/pallas_call | solution.py:23
  320.0 25.8 %shard_map.108 = (bf16[16,256,1792]{2,1,0:T(8,128)(2,1)}, bf16[16,256,1792]{2,1,0:T(8,128)(2,1)}) custom-call(s32[8]{0:T(128)} %iota_xor_fusion.refs_0_, bf16[256,4096]{1,0:T(8,128)(2,1)} %collective-permute-done.15.refs_1_.refs_11_, bf16[256,4096]{1,0:T(8,128)(2,1)} %copy-done.3, ...), custom_call_target="tpu_custom_call", output_to_operand_aliasing={{0}: (14, {}), {1}: (15, {})} | custom-call | flops 15032385536 | bytes 37748736 | tf_op jit(solution)/shard_map/pallas_call | solution.py:23
  345.8 37.6 %shard_map.109 = (bf16[2,256,2048]{2,1,0:T(8,128)(2,1)}, bf16[2,256,2048]{2,1,0:T(8,128)(2,1)}, bf16[2,256,2048]{2,1,0:T(8,128)(2,1)}, bf16[2,256,2048]{2,1,0:T(8,128)(2,1)}) custom-call(bf16[16,256,1792]{2,1,0:T(8,128)(2,1)} %get-tuple-element.82.refs_0_, bf16[16,256,1792]{2,1,0:T(8,128)(2,1)} %get-tuple-element.83.refs_1_, bf16[4096,1792]{1,0:T(8,128)(2,1)} %refs_3_.5, ...), custom_call_target="tpu_custom_call" | custom-call | flops 30064771072 | bytes 45088768 | tf_op jit(solution)/shard_map/pallas_call | solution.py:23
  384.4 3.3 collective-permute-done.32.refs_8_
  400.1 71.2 %shard_map.110.refs_15_ = f32[1792,4096]{1,0:T(8,128)} custom-call(bf16[1792,4096]{1,0:T(8,128)(2,1)} %shard_map.105.refs_28_.refs_0_, bf16[512,4096]{1,0:T(8,128)(2,1)} %refs_1_.3, bf16[512,4096]{1,0:T(8,128)(2,1)} %collective-permute-done.4.refs_3_.refs_4_.refs_2_, bf16[256,4096]{1,0:T(8,128)(2,1)} %collective-permute-done.2.refs_1_.refs_3_, ...), custom_call_target="tpu_custom_call" | custom-call | flops 60129542144 | bytes 77594624 | tf_op jit(solution)/shard_map/pallas_call | solution.py:23
  471.9 11.0 %collective-permute-done.25.refs_3_ = bf16[2,256,2048]{2,1,0:T(8,128)(2,1)} collective-permute-done((bf16[2,256,2048]{2,1,0:T(8,128)(2,1)}, bf16[2,256,2048]{2,1,0:T(8,128)(2,1)}, u32[]{:S(2)}, u32[]{:S(2)}) %collective-permute-start.25) | collective-permute-done | bytes 2097184 | tf_op jit(solution)/shard_map/ppermute | solution.py:221
  483.7 5.2 collective-permute-done.28.refs_7_
  490.9 71.0 %shard_map.111.refs_8_ = f32[4096,1792]{1,0:T(8,128)} custom-call(bf16[4096,1792]{1,0:T(8,128)(2,1)} %bitcast.40, bf16[256,4096]{1,0:T(8,128)(2,1)} %collective-permute-done.6.refs_1_, bf16[256,4096]{1,0:T(8,128)(2,1)} %collective-permute-done.7.refs_2_, bf16[256,4096]{1,0:T(8,128)(2,1)} %collective-permute-done.29.refs_3_, ...), custom_call_target="tpu_custom_call" | custom-call | flops 60129542144 | bytes 77594624 | tf_op jit(solution)/shard_map/pallas_call | solution.py:23
  561.9 6.0 shard_map.112
  567.8 5.9 shard_map.113
  577.8 71.2 %shard_map.114.refs_10_ = f32[4096,1792]{1,0:T(8,128)} custom-call(bf16[4096,1792]{1,0:T(8,128)(2,1)} %bitcast.41, bf16[256,4096]{1,0:T(8,128)(2,1)} %collective-permute-done.6.refs_1_, bf16[256,4096]{1,0:T(8,128)(2,1)} %collective-permute-done.7.refs_2_, bf16[256,4096]{1,0:T(8,128)(2,1)} %collective-permute-done.29.refs_3_, ...), custom_call_target="tpu_custom_call" | custom-call | flops 60129542144 | bytes 77594624 | tf_op jit(solution)/shard_map/pallas_call | solution.py:23
  649.0 17.9 %collective-permute-done.40.refs_8_ = f32[256,2048]{1,0:T(8,128)} collective-permute-done((f32[256,2048]{1,0:T(8,128)}, f32[256,2048]{1,0:T(8,128)}, u32[]{:S(2)}, u32[]{:S(2)}) %collective-permute-start.40) | collective-permute-done | bytes 2097184 | tf_op jit(solution)/shard_map/ppermute | solution.py:221
  667.0 6.5 shard_map.115.refs_10_
  673.5 38.4 %collective-permute-done.38.refs_8_ = f32[256,2048]{1,0:T(8,128)} collective-permute-done((f32[256,2048]{1,0:T(8,128)}, f32[256,2048]{1,0:T(8,128)}, u32[]{:S(2)}, u32[]{:S(2)}) %collective-permute-start.38) | collective-permute-done | bytes 2097184 | tf_op jit(solution)/shard_map/ppermute | solution.py:221
  711.9 6.6 shard_map.116
  (88 shorter events, 38.0 us)
Async XLA Ops:
  6.2 95.5 %collective-permute-start.3 = (bf16[256,4096]{1,0:T(8,128)(2,1)}, bf16[256,4096]{1,0:T(8,128)(2,1)}, u32[]{:S(2)}, u32[]{:S(2)}) collective-permute-start(bf16[256,4096]{1,0:T(8,128)(2,1)} %get-tuple-element.111), channel_id=1, source_target_pairs={{0,4},{1,5},{2,6},{3,7},{4,0},{5,1},{6,2},{7,3}} | collective-permute-start | bytes 6291464 | tf_op jit(solution)/shard_map/ppermute | solution.py:221
  8.7 130.6 %collective-permute-start = (bf16[256,4096]{1,0:T(8,128)(2,1)}, bf16[256,4096]{1,0:T(8,128)(2,1)S(1)}, u32[]{:S(2)}, u32[]{:S(2)}) collective-permute-start(bf16[256,4096]{1,0:T(8,128)(2,1)} %get-tuple-element.111), channel_id=1, source_target_pairs={{0,2},{1,3},{2,0},{3,1},{4,6},{5,7},{6,4},{7,5}} | collective-permute-start | bytes 6291464 | tf_op jit(solution)/shard_map/ppermute | solution.py:221
  10.2 91.5 %collective-permute-start.2 = (bf16[256,4096]{1,0:T(8,128)(2,1)}, bf16[256,4096]{1,0:T(8,128)(2,1)}, u32[]{:S(2)}, u32[]{:S(2)}) collective-permute-start(bf16[256,4096]{1,0:T(8,128)(2,1)} %get-tuple-element.110), channel_id=1, source_target_pairs={{0,2},{1,3},{2,0},{3,1},{4,6},{5,7},{6,4},{7,5}} | collective-permute-start | bytes 6291464 | tf_op jit(solution)/shard_map/ppermute | solution.py:221
  10.8 128.6 %collective-permute-start.1 = (bf16[256,4096]{1,0:T(8,128)(2,1)}, bf16[256,4096]{1,0:T(8,128)(2,1)}, u32[]{:S(2)}, u32[]{:S(2)}) collective-permute-start(bf16[256,4096]{1,0:T(8,128)(2,1)} %get-tuple-element.110), channel_id=1, source_target_pairs={{0,4},{1,5},{2,6},{3,7},{4,0},{5,1},{6,2},{7,3}} | collective-permute-start | bytes 6291464 | tf_op jit(solution)/shard_map/ppermute | solution.py:221
  152.8 92.0 %collective-permute-start.6 = (bf16[256,4096]{1,0:T(8,128)(2,1)}, bf16[256,4096]{1,0:T(8,128)(2,1)}, u32[]{:S(2)}, u32[]{:S(2)}) collective-permute-start(bf16[256,4096]{1,0:T(8,128)(2,1)} %get-tuple-element.67), channel_id=1, source_target_pairs={{0,2},{1,3},{2,0},{3,1},{4,6},{5,7},{6,4},{7,5}} | collective-permute-start | bytes 6291464 | tf_op jit(solution)/shard_map/ppermute | solution.py:221
  153.1 162.9 %collective-permute-start.8 = (bf16[256,4096]{1,0:T(8,128)(2,1)}, bf16[256,4096]{1,0:T(8,128)(2,1)}, u32[]{:S(2)}, u32[]{:S(2)}) collective-permute-start(bf16[256,4096]{1,0:T(8,128)(2,1)} %get-tuple-element.67), channel_id=1, source_target_pairs={{0,4},{1,5},{2,6},{3,7},{4,0},{5,1},{6,2},{7,3}} | collective-permute-start | bytes 6291464 | tf_op jit(solution)/shard_map/ppermute | solution.py:221
  154.9 161.1 %collective-permute-start.7 = (bf16[256,4096]{1,0:T(8,128)(2,1)}, bf16[256,4096]{1,0:T(8,128)(2,1)}, u32[]{:S(2)}, u32[]{:S(2)}) collective-permute-start(bf16[256,4096]{1,0:T(8,128)(2,1)} %get-tuple-element.68), channel_id=1, source_target_pairs={{0,2},{1,3},{2,0},{3,1},{4,6},{5,7},{6,4},{7,5}} | collective-permute-start | bytes 6291464 | tf_op jit(solution)/shard_map/ppermute | solution.py:221
  203.4 112.6 %collective-permute-start.9 = (bf16[256,4096]{1,0:T(8,128)(2,1)}, bf16[256,4096]{1,0:T(8,128)(2,1)}, u32[]{:S(2)}, u32[]{:S(2)}) collective-permute-start(bf16[256,4096]{1,0:T(8,128)(2,1)} %get-tuple-element.68), channel_id=1, source_target_pairs={{0,4},{1,5},{2,6},{3,7},{4,0},{5,1},{6,2},{7,3}} | collective-permute-start | bytes 6291464 | tf_op jit(solution)/shard_map/ppermute | solution.py:221
  203.9 115.6 %collective-permute-start.17 = (bf16[256,4096]{1,0:T(8,128)(2,1)}, bf16[256,4096]{1,0:T(8,128)(2,1)}, u32[]{:S(2)}, u32[]{:S(2)}) collective-permute-start(bf16[256,4096]{1,0:T(8,128)(2,1)} %collective-permute-done.15.refs_1_.refs_11_), channel_id=1, source_target_pairs={{0,1},{1,0},{2,3},{3,2},{4,5},{5,4},{6,7},{7,6}} | collective-permute-start | bytes 6291464 | tf_op jit(solution)/shard_map/ppermute | solution.py:221
  387.7 83.6 %collective-permute-start.33 = (bf16[512,4096]{1,0:T(8,128)(2,1)}, bf16[512,4096]{1,0:T(8,128)(2,1)}, u32[]{:S(2)}, u32[]{:S(2)}) collective-permute-start(bf16[512,4096]{1,0:T(8,128)(2,1)} %refs_9_.5), channel_id=1, source_target_pairs={{0,1},{1,0},{2,3},{3,2},{4,5},{5,4},{6,7},{7,6}} | collective-permute-start | bytes 12582920 | tf_op jit(solution)/shard_map/ppermute | solution.py:221
  390.7 81.0 %collective-permute-start.24 = (bf16[2,256,2048]{2,1,0:T(8,128)(2,1)}, bf16[2,256,2048]{2,1,0:T(8,128)(2,1)}, u32[]{:S(2)}, u32[]{:S(2)}) collective-permute-start(bf16[2,256,2048]{2,1,0:T(8,128)(2,1)} %get-tuple-element.84.refs_15_), channel_id=1, source_target_pairs={{0,2},{1,3},{2,0},{3,1},{4,6},{5,7},{6,4},{7,5}} | collective-permute-start | bytes 6291464 | tf_op jit(solution)/shard_map/ppermute | solution.py:221
  393.9 89.0 %collective-permute-start.25 = (bf16[2,256,2048]{2,1,0:T(8,128)(2,1)}, bf16[2,256,2048]{2,1,0:T(8,128)(2,1)}, u32[]{:S(2)}, u32[]{:S(2)}) collective-permute-start(bf16[2,256,2048]{2,1,0:T(8,128)(2,1)} %get-tuple-element.92), channel_id=1, source_target_pairs={{0,3},{1,2},{2,1},{3,0},{4,7},{5,6},{6,5},{7,4}} | collective-permute-start | bytes 6291464 | tf_op jit(solution)/shard_map/ppermute | solution.py:221
  396.9 86.5 %collective-permute-start.27 = (bf16[2,256,2048]{2,1,0:T(8,128)(2,1)}, bf16[2,256,2048]{2,1,0:T(8,128)(2,1)}, u32[]{:S(2)}, u32[]{:S(2)}) collective-permute-start(bf16[2,256,2048]{2,1,0:T(8,128)(2,1)} %get-tuple-element.95), channel_id=1, source_target_pairs={{0,4},{1,5},{2,6},{3,7},{4,0},{5,1},{6,2},{7,3}} | collective-permute-start | bytes 6291464 | tf_op jit(solution)/shard_map/ppermute | solution.py:221
  399.9 89.1 %collective-permute-start.28 = (bf16[2,256,2048]{2,1,0:T(8,128)(2,1)}, bf16[2,256,2048]{2,1,0:T(8,128)(2,1)}, u32[]{:S(2)}, u32[]{:S(2)}) collective-permute-start(bf16[2,256,2048]{2,1,0:T(8,128)(2,1)} %get-tuple-element.96), channel_id=1, source_target_pairs={{0,5},{1,4},{2,7},{3,6},{4,1},{5,0},{6,3},{7,2}} | collective-permute-start | bytes 6291464 | tf_op jit(solution)/shard_map/ppermute | solution.py:221
  471.3 102.3 %collective-permute-start.20 = (bf16[2,256,2048]{2,1,0:T(8,128)(2,1)}, bf16[2,256,2048]{2,1,0:T(8,128)(2,1)S(1)}, u32[]{:S(2)}, u32[]{:S(2)}) collective-permute-start(bf16[2,256,2048]{2,1,0:T(8,128)(2,1)} %get-tuple-element.87), channel_id=1, source_target_pairs={{0,1},{1,0},{2,3},{3,2},{4,5},{5,4},{6,7},{7,6}} | collective-permute-start | bytes 6291464 | tf_op jit(solution)/shard_map/ppermute | solution.py:221
  471.7 102.0 %collective-permute-start.5 = (bf16[2,256,2048]{2,1,0:T(8,128)(2,1)}, bf16[2,256,2048]{2,1,0:T(8,128)(2,1)}, u32[]{:S(2)}, u32[]{:S(2)}) collective-permute-start(bf16[2,256,2048]{2,1,0:T(8,128)(2,1)} %get-tuple-element.66), channel_id=1, source_target_pairs={{0,1},{1,0},{2,3},{3,2},{4,5},{5,4},{6,7},{7,6}} | collective-permute-start | bytes 6291464 | tf_op jit(solution)/shard_map/ppermute | solution.py:221
  482.8 92.4 %collective-permute-start.14 = (bf16[2,256,2048]{2,1,0:T(8,128)(2,1)}, bf16[2,256,2048]{2,1,0:T(8,128)(2,1)}, u32[]{:S(2)}, u32[]{:S(2)}) collective-permute-start(bf16[2,256,2048]{2,1,0:T(8,128)(2,1)} %get-tuple-element.77.refs_16_), channel_id=1, source_target_pairs={{0,2},{1,3},{2,0},{3,1},{4,6},{5,7},{6,4},{7,5}} | collective-permute-start | bytes 6291464 | tf_op jit(solution)/shard_map/ppermute | solution.py:221
  483.4 92.4 %collective-permute-start.21 = (bf16[2,256,2048]{2,1,0:T(8,128)(2,1)}, bf16[2,256,2048]{2,1,0:T(8,128)(2,1)}, u32[]{:S(2)}, u32[]{:S(2)}) collective-permute-start(bf16[2,256,2048]{2,1,0:T(8,128)(2,1)} %get-tuple-element.88), channel_id=1, source_target_pairs={{0,4},{1,5},{2,6},{3,7},{4,0},{5,1},{6,2},{7,3}} | collective-permute-start | bytes 6291464 | tf_op jit(solution)/shard_map/ppermute | solution.py:221
  489.0 88.3 %collective-permute-start.19 = (bf16[2,256,2048]{2,1,0:T(8,128)(2,1)}, bf16[2,256,2048]{2,1,0:T(8,128)(2,1)}, u32[]{:S(2)}, u32[]{:S(2)}) collective-permute-start(bf16[2,256,2048]{2,1,0:T(8,128)(2,1)} %get-tuple-element.85), channel_id=1, source_target_pairs={{0,3},{1,2},{2,1},{3,0},{4,7},{5,6},{6,5},{7,4}} | collective-permute-start | bytes 6291464 | tf_op jit(solution)/shard_map/ppermute | solution.py:221
  573.7 75.3 %collective-permute-start.22 = (bf16[2,256,2048]{2,1,0:T(8,128)(2,1)}, bf16[2,256,2048]{2,1,0:T(8,128)(2,1)}, u32[]{:S(2)}, u32[]{:S(2)}) collective-permute-start(bf16[2,256,2048]{2,1,0:T(8,128)(2,1)} %get-tuple-element.89), channel_id=1, source_target_pairs={{0,5},{1,4},{2,7},{3,6},{4,1},{5,0},{6,3},{7,2}} | collective-permute-start | bytes 6291464 | tf_op jit(solution)/shard_map/ppermute | solution.py:221
  573.7 93.2 %collective-permute-start.40 = (f32[256,2048]{1,0:T(8,128)}, f32[256,2048]{1,0:T(8,128)}, u32[]{:S(2)}, u32[]{:S(2)}) collective-permute-start(f32[256,2048]{1,0:T(8,128)} %get-tuple-element.104.refs_8_), channel_id=1, source_target_pairs={{0,4},{1,5},{2,6},{3,7},{4,0},{5,1},{6,2},{7,3}} | collective-permute-start | bytes 6291464 | tf_op jit(solution)/shard_map/ppermute | solution.py:221
  575.2 91.7 %collective-permute-start.41 = (f32[256,2048]{1,0:T(8,128)}, f32[256,2048]{1,0:T(8,128)}, u32[]{:S(2)}, u32[]{:S(2)}) collective-permute-start(f32[256,2048]{1,0:T(8,128)} %get-tuple-element.107), channel_id=1, source_target_pairs={{0,2},{1,3},{2,0},{3,1},{4,6},{5,7},{6,4},{7,5}} | collective-permute-start | bytes 6291464 | tf_op jit(solution)/shard_map/ppermute | solution.py:221
  575.8 136.1 %collective-permute-start.38 = (f32[256,2048]{1,0:T(8,128)}, f32[256,2048]{1,0:T(8,128)}, u32[]{:S(2)}, u32[]{:S(2)}) collective-permute-start(f32[256,2048]{1,0:T(8,128)} %get-tuple-element.105.refs_15_), channel_id=1, source_target_pairs={{0,4},{1,5},{2,6},{3,7},{4,0},{5,1},{6,2},{7,3}} | collective-permute-start | bytes 6291464 | tf_op jit(solution)/shard_map/ppermute | solution.py:221
  577.3 134.6 %collective-permute-start.39 = (f32[256,2048]{1,0:T(8,128)}, f32[256,2048]{1,0:T(8,128)}, u32[]{:S(2)}, u32[]{:S(2)}) collective-permute-start(f32[256,2048]{1,0:T(8,128)} %get-tuple-element.106), channel_id=1, source_target_pairs={{0,2},{1,3},{2,0},{3,1},{4,6},{5,7},{6,4},{7,5}} | collective-permute-start | bytes 6291464 | tf_op jit(solution)/shard_map/ppermute | solution.py:221
  (23 other events, 915.3 us)

commit v2 on v1

--- a/solution.py
+++ b/solution.py
@@ -11,7 +11,7 @@
 CHUNKS = 2
 NT = (((1,), (1,)), ((), ()))
 NN = (((1,), (0,)), ((), ()))
-VMEM_LIMIT = 60 * 1024 * 1024
+VMEM_LIMIT = 67_043_328
 
 
 def _call(body, args, *, flops, nbytes, grid, in_specs, out_specs, out_shape, place=None, deps=(), aliases=None):
@@ -55,6 +55,19 @@
 def _rows_of(refs):
     vals = [_value(r) for r in refs]
     return vals[0] if len(vals) == 1 else jnp.concatenate(vals, axis=0)
+
+
+def _copy_body(in_ref, out_ref):
+    out_ref[...] = in_ref[...]
+
+
+def _copy_half(a, h, deps, step=64):
+    tok, hidden = a.shape
+    steps = tok // CHUNKS // step
+    return _call(
+        _copy_body, (a,), flops=tok * hidden, nbytes=2 * tok * hidden, deps=deps, grid=(steps,),
+        in_specs=[_along((step, hidden), 0, 0, 0, offset=h * steps)], out_specs=_along((step, hidden), 0, 0, 0),
+        out_shape=jax.ShapeDtypeStruct((tok // CHUNKS, hidden), a.dtype))
 
 
 def _z_body(ug_ref, uu_ref, *rest):
@@ -231,7 +244,8 @@
         hs = range(CHUNKS)
 
         dy_mate = send(dy_loc, 1)
-        halves = [dy_loc[:rows], dy_loc[rows:]]
+        first = _copy_half(dy_loc, 0, ())
+        halves = [first, _copy_half(dy_loc, 1, (first,))]
         dy_x, dy_y = [None, None], [None, None]
         for h in hs:
             dy_x[h] = send(halves[h], 2)

time: 727 us -> 692 us (0.952)
  waiting for transfers between devices: 177 us -> 134 us
    ppermute x42, waiting for transfers between devices: 177 us -> 134 us  [send(): return lax.ppermute(value, 'tp', [(d, d ^ away) for d in range(group)])]
    pallas_call x15 -> x17, Pallas kernels: 504 us -> 511 us  [_call(): pl.pallas_call(kernel, grid_spec=pltpu.PrefetchScalarGridSpec(num_scalar_...]
  transfers between devices with their start and end apart: 42 -> 42, of which waited for: 11 -> 13; matrix products, arithmetic and copies ran while one was open for 1% -> 1% of each run, Pallas kernels for 69% -> 74%
where the time goes in v2:
time: 692 us; the launch traced here: 684 us
  Pallas kernels  511 us (74%)
  waiting for transfers between devices  134 us (19%)
  starting transfers between devices  31.6 us (5%)
    pallas_call x17, Pallas kernels, _call(): pl.pallas_call(kernel, grid_spec=pltpu.PrefetchScalarGridSpec(num_scalar_...  511 us
    ppermute x42, waiting for transfers between devices, send(): return lax.ppermute(value, 'tp', [(d, d ^ away) for d in range(group)])  134 us
    ppermute x42, starting transfers between devices, send(): return lax.ppermute(value, 'tp', [(d, d ^ away) for d in range(group)])  31.6 us
  transfers between devices with their start and end apart: 42, of which 13 were waited for; matrix products, arithmetic and copies ran while one was open for 1% of the time, Pallas kernels for 74%

profile of v2, /device:TPU:0, one launch (start us, length us, event | category | flops | bytes accessed | tf_op | source)
XLA Modules:
  0.0 683.6 jit_solution(6912584229040792418)
XLA Ops:
  1.5 3.8 shard_map.102.refs_1_
  7.8 3.8 shard_map.103
  14.2 10.4 %shard_map.104.refs_14_.refs_3_ = bf16[1792,4096]{1,0:T(8,128)(2,1)} custom-call(s32[8]{0:T(128)} %iota_xor_fusion.refs_0_, bf16[8,2,256,1792]{3,2,1,0:T(8,128)(2,1)} %bitcast.4, bf16[8,2,256,1792]{3,2,1,0:T(8,128)(2,1)} %bitcast.22), custom_call_target="tpu_custom_call" | custom-call | flops 29360128 | bytes 22020096 | tf_op jit(solution)/shard_map/pallas_call | solution.py:23
  24.6 25.7 %shard_map.105 = (bf16[16,256,1792]{2,1,0:T(8,128)(2,1)}, bf16[16,256,1792]{2,1,0:T(8,128)(2,1)}) custom-call(s32[8]{0:T(128)} %iota_xor_fusion.refs_0_, bf16[512,4096]{1,0:T(8,128)(2,1)} %refs_1_.3, bf16[512,4096]{1,0:T(8,128)(2,1)} %refs_1_.3, bf16[512,4096]{1,0:T(8,128)(2,1)} %collective-permute-done.4.refs_3_.refs_4_.refs_2_, ...), custom_call_target="tpu_custom_call" | custom-call | flops 15032385536 | bytes 37748736 | tf_op jit(solution)/shard_map/pallas_call | solution.py:23
  50.3 4.7 fusion
  55.0 5.3 collective-permute-done.3.refs_6_.refs_8_
  60.4 37.6 %shard_map.106 = (bf16[2,256,2048]{2,1,0:T(8,128)(2,1)}, bf16[2,256,2048]{2,1,0:T(8,128)(2,1)}, bf16[2,256,2048]{2,1,0:T(8,128)(2,1)}, bf16[2,256,2048]{2,1,0:T(8,128)(2,1)}) custom-call(bf16[16,256,1792]{2,1,0:T(8,128)(2,1)} %get-tuple-element.61.refs_0_.refs_26_, bf16[16,256,1792]{2,1,0:T(8,128)(2,1)} %get-tuple-element.62.refs_1_.refs_27_, ...), custom_call_target="tpu_custom_call" | custom-call | flops 30064771072 | bytes 45088768 | tf_op jit(solution)/shard_map/pallas_call | solution.py:23
  99.3 5.2 collective-permute-done.1.refs_6_.refs_5_.refs_7_
  107.1 10.4 %shard_map.107.refs_28_.refs_0_ = bf16[1792,4096]{1,0:T(8,128)(2,1)} custom-call(s32[8]{0:T(128)} %iota_xor_fusion.refs_0_, bf16[8,2,256,1792]{3,2,1,0:T(8,128)(2,1)} %bitcast.9, bf16[8,2,256,1792]{3,2,1,0:T(8,128)(2,1)} %bitcast.27, bf16[1792,4096]{1,0:T(8,128)(2,1)} %shard_map.104.refs_14_.refs_3_, ...), custom_call_target="tpu_custom_call", output_to_operand_aliasing={{}: (3, {})} | custom-call | flops 29360128 | bytes 22020096 | tf_op jit(solution)/shard_map/pallas_call | solution.py:23
  120.3 47.0 %shard_map.108 = (bf16[16,256,1792]{2,1,0:T(8,128)(2,1)}, bf16[16,256,1792]{2,1,0:T(8,128)(2,1)}) custom-call(s32[8]{0:T(128)} %iota_xor_fusion.refs_0_, bf16[256,4096]{1,0:T(8,128)(2,1)} %collective-permute-done.2.refs_1_.refs_3_, bf16[256,4096]{1,0:T(8,128)(2,1)} %collective-permute-done.refs_5_.refs_2_.refs_4_, ...), custom_call_target="tpu_custom_call", output_to_operand_aliasing={{0}: (26, {}), {1}: (27, {})} | custom-call | flops 30064771072 | bytes 60817408 | tf_op jit(solution)/shard_map/pallas_call | solution.py:23
  169.1 42.1 %collective-permute-done.6.refs_1_ = bf16[256,4096]{1,0:T(8,128)(2,1)} collective-permute-done((bf16[256,4096]{1,0:T(8,128)(2,1)}, bf16[256,4096]{1,0:T(8,128)(2,1)}, u32[]{:S(2)}, u32[]{:S(2)}) %collective-permute-start.6) | collective-permute-done | bytes 2097184 | tf_op jit(solution)/shard_map/ppermute | solution.py:234
  211.2 71.1 %shard_map.109 = (bf16[2,256,2048]{2,1,0:T(8,128)(2,1)}, bf16[2,256,2048]{2,1,0:T(8,128)(2,1)}, bf16[2,256,2048]{2,1,0:T(8,128)(2,1)}, bf16[2,256,2048]{2,1,0:T(...) custom-call(bf16[16,256,1792]{2,1,0:T(8,128)(2,1)} %get-tuple-elemen, ...), custom_call_target="tpu_custom_call" | custom-call | flops 60129542144 | bytes 60817408 | tf_op jit(solution)/shard_map/pallas_call | solution.py:23
  284.0 25.7 %shard_map.110 = (bf16[16,256,1792]{2,1,0:T(8,128)(2,1)}, bf16[16,256,1792]{2,1,0:T(8,128)(2,1)}) custom-call(s32[8]{0:T(128)} %iota_xor_fusion.refs_0_, bf16[256,4096]{1,0:T(8,128)(2,1)} %collective-permute-done.15.refs_1_.refs_11_, bf16[256,4096]{1,0:T(8,128)(2,1)} %collective-permute-done.16.refs_2_.refs_12_, ...), custom_call_target="tpu_custom_call", output_to_operand_aliasing={{0}: (14, {}), {1}: (15, {})} | custom-call | flops 15032385536 | bytes 37748736 | tf_op jit(solution)/shard_map/pallas_call | solution.py:23
  309.7 37.6 %shard_map.111 = (bf16[2,256,2048]{2,1,0:T(8,128)(2,1)}, bf16[2,256,2048]{2,1,0:T(8,128)(2,1)}, bf16[2,256,2048]{2,1,0:T(8,128)(2,1)}, bf16[2,256,2048]{2,1,0:T(8,128)(2,1)}) custom-call(bf16[16,256,1792]{2,1,0:T(8,128)(2,1)} %get-tuple-element.82.refs_0_, bf16[16,256,1792]{2,1,0:T(8,128)(2,1)} %get-tuple-element.83.refs_1_, bf16[4096,1792]{1,0:T(8,128)(2,1)} %refs_3_.5, ...), custom_call_target="tpu_custom_call" | custom-call | flops 30064771072 | bytes 45088768 | tf_op jit(solution)/shard_map/pallas_call | solution.py:23
  365.2 71.2 %shard_map.112.refs_15_ = f32[1792,4096]{1,0:T(8,128)} custom-call(bf16[1792,4096]{1,0:T(8,128)(2,1)} %shard_map.107.refs_28_.refs_0_, bf16[512,4096]{1,0:T(8,128)(2,1)} %refs_1_.3, bf16[512,4096]{1,0:T(8,128)(2,1)} %collective-permute-done.4.refs_3_.refs_4_.refs_2_, bf16[256,4096]{1,0:T(8,128)(2,1)} %collective-permute-done.2.refs_1_.refs_3_, ...), custom_call_target="tpu_custom_call" | custom-call | flops 60129542144 | bytes 77594624 | tf_op jit(solution)/shard_map/pallas_call | solution.py:23
  437.0 9.9 %collective-permute-done.25.refs_3_ = bf16[2,256,2048]{2,1,0:T(8,128)(2,1)} collective-permute-done((bf16[2,256,2048]{2,1,0:T(8,128)(2,1)}, bf16[2,256,2048]{2,1,0:T(8,128)(2,1)}, u32[]{:S(2)}, u32[]{:S(2)}) %collective-permute-start.25) | collective-permute-done | bytes 2097184 | tf_op jit(solution)/shard_map/ppermute | solution.py:234
  455.9 71.0 %shard_map.113.refs_8_ = f32[4096,1792]{1,0:T(8,128)} custom-call(bf16[4096,1792]{1,0:T(8,128)(2,1)} %bitcast.40, bf16[256,4096]{1,0:T(8,128)(2,1)} %collective-permute-done.6.refs_1_, bf16[256,4096]{1,0:T(8,128)(2,1)} %collective-permute-done.7.refs_2_, bf16[256,4096]{1,0:T(8,128)(2,1)} %collective-permute-done.29.refs_3_, ...), custom_call_target="tpu_custom_call" | custom-call | flops 60129542144 | bytes 77594624 | tf_op jit(solution)/shard_map/pallas_call | solution.py:23
  526.9 5.9 shard_map.114
  532.8 5.9 shard_map.115
  542.8 71.2 %shard_map.116.refs_10_ = f32[4096,1792]{1,0:T(8,128)} custom-call(bf16[4096,1792]{1,0:T(8,128)(2,1)} %bitcast.41, bf16[256,4096]{1,0:T(8,128)(2,1)} %collective-permute-done.6.refs_1_, bf16[256,4096]{1,0:T(8,128)(2,1)} %collective-permute-done.7.refs_2_, bf16[256,4096]{1,0:T(8,128)(2,1)} %collective-permute-done.29.refs_3_, ...), custom_call_target="tpu_custom_call" | custom-call | flops 60129542144 | bytes 77594624 | tf_op jit(solution)/shard_map/pallas_call | solution.py:23
  614.1 17.9 %collective-permute-done.40.refs_8_ = f32[256,2048]{1,0:T(8,128)} collective-permute-done((f32[256,2048]{1,0:T(8,128)}, f32[256,2048]{1,0:T(8,128)}, u32[]{:S(2)}, u32[]{:S(2)}) %collective-permute-start.40) | collective-permute-done | bytes 2097184 | tf_op jit(solution)/shard_map/ppermute | solution.py:234
  632.0 6.5 shard_map.117.refs_10_
  638.5 38.3 %collective-permute-done.38.refs_8_ = f32[256,2048]{1,0:T(8,128)} collective-permute-done((f32[256,2048]{1,0:T(8,128)}, f32[256,2048]{1,0:T(8,128)}, u32[]{:S(2)}, u32[]{:S(2)}) %collective-permute-start.38) | collective-permute-done | bytes 2097184 | tf_op jit(solution)/shard_map/ppermute | solution.py:234
  676.9 6.5 shard_map.118
  (79 shorter events, 47.8 us)
Async XLA Ops:
  13.1 86.2 %collective-permute-start = (bf16[256,4096]{1,0:T(8,128)(2,1)}, bf16[256,4096]{1,0:T(8,128)(2,1)}, u32[]{:S(2)}, u32[]{:S(2)}) collective-permute-start(bf16[256,4096]{1,0:T(8,128)(2,1)} %shard_map.103), channel_id=1, source_target_pairs={{0,2},{1,3},{2,0},{3,1},{4,6},{5,7},{6,4},{7,5}} | collective-permute-start | bytes 6291464 | tf_op jit(solution)/shard_map/ppermute | solution.py:234
  13.6 90.9 %collective-permute-start.1 = (bf16[256,4096]{1,0:T(8,128)(2,1)}, bf16[256,4096]{1,0:T(8,128)(2,1)}, u32[]{:S(2)}, u32[]{:S(2)}) collective-permute-start(bf16[256,4096]{1,0:T(8,128)(2,1)} %shard_map.102.refs_1_), channel_id=1, source_target_pairs={{0,4},{1,5},{2,6},{3,7},{4,0},{5,1},{6,2},{7,3}} | collective-permute-start | bytes 6291464 | tf_op jit(solution)/shard_map/ppermute | solution.py:234
  118.0 93.2 %collective-permute-start.6 = (bf16[256,4096]{1,0:T(8,128)(2,1)}, bf16[256,4096]{1,0:T(8,128)(2,1)}, u32[]{:S(2)}, u32[]{:S(2)}) collective-permute-start(bf16[256,4096]{1,0:T(8,128)(2,1)} %get-tuple-element.67), channel_id=1, source_target_pairs={{0,2},{1,3},{2,0},{3,1},{4,6},{5,7},{6,4},{7,5}} | collective-permute-start | bytes 6291464 | tf_op jit(solution)/shard_map/ppermute | solution.py:234
  119.5 162.9 %collective-permute-start.8 = (bf16[256,4096]{1,0:T(8,128)(2,1)}, bf16[256,4096]{1,0:T(8,128)(2,1)}, u32[]{:S(2)}, u32[]{:S(2)}) collective-permute-start(bf16[256,4096]{1,0:T(8,128)(2,1)} %get-tuple-element.67), channel_id=1, source_target_pairs={{0,4},{1,5},{2,6},{3,7},{4,0},{5,1},{6,2},{7,3}} | collective-permute-start | bytes 6291464 | tf_op jit(solution)/shard_map/ppermute | solution.py:234
  120.0 162.3 %collective-permute-start.7 = (bf16[256,4096]{1,0:T(8,128)(2,1)}, bf16[256,4096]{1,0:T(8,128)(2,1)}, u32[]{:S(2)}, u32[]{:S(2)}) collective-permute-start(bf16[256,4096]{1,0:T(8,128)(2,1)} %get-tuple-element.68), channel_id=1, source_target_pairs={{0,2},{1,3},{2,0},{3,1},{4,6},{5,7},{6,4},{7,5}} | collective-permute-start | bytes 6291464 | tf_op jit(solution)/shard_map/ppermute | solution.py:234
  167.4 115.0 %collective-permute-start.9 = (bf16[256,4096]{1,0:T(8,128)(2,1)}, bf16[256,4096]{1,0:T(8,128)(2,1)}, u32[]{:S(2)}, u32[]{:S(2)}) collective-permute-start(bf16[256,4096]{1,0:T(8,128)(2,1)} %get-tuple-element.68), channel_id=1, source_target_pairs={{0,4},{1,5},{2,6},{3,7},{4,0},{5,1},{6,2},{7,3}} | collective-permute-start | bytes 6291464 | tf_op jit(solution)/shard_map/ppermute | solution.py:234
  169.1 114.3 %collective-permute-start.17 = (bf16[256,4096]{1,0:T(8,128)(2,1)}, bf16[256,4096]{1,0:T(8,128)(2,1)}, u32[]{:S(2)}, u32[]{:S(2)}) collective-permute-start(bf16[256,4096]{1,0:T(8,128)(2,1)} %collective-permute-done.15.refs_1_.refs_11_), channel_id=1, source_target_pairs={{0,1},{1,0},{2,3},{3,2},{4,5},{5,4},{6,7},{7,6}} | collective-permute-start | bytes 6291464 | tf_op jit(solution)/shard_map/ppermute | solution.py:234
  211.2 72.3 %collective-permute-start.18 = (bf16[256,4096]{1,0:T(8,128)(2,1)}, bf16[256,4096]{1,0:T(8,128)(2,1)}, u32[]{:S(2)}, u32[]{:S(2)}) collective-permute-start(bf16[256,4096]{1,0:T(8,128)(2,1)} %collective-permute-done.16.refs_2_.refs_12_), channel_id=1, source_target_pairs={{0,1},{1,0},{2,3},{3,2},{4,5},{5,4},{6,7},{7,6}} | collective-permute-start | bytes 6291464 | tf_op jit(solution)/shard_map/ppermute | solution.py:234
  282.9 64.9 %collective-permute-start.29 = (bf16[256,4096]{1,0:T(8,128)(2,1)}, bf16[256,4096]{1,0:T(8,128)(2,1)}, u32[]{:S(2)}, u32[]{:S(2)}) collective-permute-start(bf16[256,4096]{1,0:T(8,128)(2,1)} %collective-permute-done.6.refs_1_), channel_id=1, source_target_pairs={{0,1},{1,0},{2,3},{3,2},{4,5},{5,4},{6,7},{7,6}} | collective-permute-start | bytes 6291464 | tf_op jit(solution)/shard_map/ppermute | solution.py:234
  351.8 84.6 %collective-permute-start.33 = (bf16[512,4096]{1,0:T(8,128)(2,1)}, bf16[512,4096]{1,0:T(8,128)(2,1)}, u32[]{:S(2)}, u32[]{:S(2)}) collective-permute-start(bf16[512,4096]{1,0:T(8,128)(2,1)} %refs_9_.5), channel_id=1, source_target_pairs={{0,1},{1,0},{2,3},{3,2},{4,5},{5,4},{6,7},{7,6}} | collective-permute-start | bytes 12582920 | tf_op jit(solution)/shard_map/ppermute | solution.py:234
  354.8 82.0 %collective-permute-start.24 = (bf16[2,256,2048]{2,1,0:T(8,128)(2,1)}, bf16[2,256,2048]{2,1,0:T(8,128)(2,1)}, u32[]{:S(2)}, u32[]{:S(2)}) collective-permute-start(bf16[2,256,2048]{2,1,0:T(8,128)(2,1)} %get-tuple-element.84.refs_15_), channel_id=1, source_target_pairs={{0,2},{1,3},{2,0},{3,1},{4,6},{5,7},{6,4},{7,5}} | collective-permute-start | bytes 6291464 | tf_op jit(solution)/shard_map/ppermute | solution.py:234
  357.8 89.1 %collective-permute-start.25 = (bf16[2,256,2048]{2,1,0:T(8,128)(2,1)}, bf16[2,256,2048]{2,1,0:T(8,128)(2,1)}, u32[]{:S(2)}, u32[]{:S(2)}) collective-permute-start(bf16[2,256,2048]{2,1,0:T(8,128)(2,1)} %get-tuple-element.92), channel_id=1, source_target_pairs={{0,3},{1,2},{2,1},{3,0},{4,7},{5,6},{6,5},{7,4}} | collective-permute-start | bytes 6291464 | tf_op jit(solution)/shard_map/ppermute | solution.py:234
  360.8 87.8 %collective-permute-start.27 = (bf16[2,256,2048]{2,1,0:T(8,128)(2,1)}, bf16[2,256,2048]{2,1,0:T(8,128)(2,1)}, u32[]{:S(2)}, u32[]{:S(2)}) collective-permute-start(bf16[2,256,2048]{2,1,0:T(8,128)(2,1)} %get-tuple-element.95), channel_id=1, source_target_pairs={{0,4},{1,5},{2,6},{3,7},{4,0},{5,1},{6,2},{7,3}} | collective-permute-start | bytes 6291464 | tf_op jit(solution)/shard_map/ppermute | solution.py:234
  363.8 90.0 %collective-permute-start.28 = (bf16[2,256,2048]{2,1,0:T(8,128)(2,1)}, bf16[2,256,2048]{2,1,0:T(8,128)(2,1)}, u32[]{:S(2)}, u32[]{:S(2)}) collective-permute-start(bf16[2,256,2048]{2,1,0:T(8,128)(2,1)} %get-tuple-element.96), channel_id=1, source_target_pairs={{0,5},{1,4},{2,7},{3,6},{4,1},{5,0},{6,3},{7,2}} | collective-permute-start | bytes 6291464 | tf_op jit(solution)/shard_map/ppermute | solution.py:234
  436.4 102.3 %collective-permute-start.20 = (bf16[2,256,2048]{2,1,0:T(8,128)(2,1)}, bf16[2,256,2048]{2,1,0:T(8,128)(2,1)}, u32[]{:S(2)}, u32[]{:S(2)}) collective-permute-start(bf16[2,256,2048]{2,1,0:T(8,128)(2,1)} %get-tuple-element.87), channel_id=1, source_target_pairs={{0,1},{1,0},{2,3},{3,2},{4,5},{5,4},{6,7},{7,6}} | collective-permute-start | bytes 6291464 | tf_op jit(solution)/shard_map/ppermute | solution.py:234
  436.8 101.9 %collective-permute-start.5 = (bf16[2,256,2048]{2,1,0:T(8,128)(2,1)}, bf16[2,256,2048]{2,1,0:T(8,128)(2,1)}, u32[]{:S(2)}, u32[]{:S(2)}) collective-permute-start(bf16[2,256,2048]{2,1,0:T(8,128)(2,1)} %get-tuple-element.66), channel_id=1, source_target_pairs={{0,1},{1,0},{2,3},{3,2},{4,5},{5,4},{6,7},{7,6}} | collective-permute-start | bytes 6291464 | tf_op jit(solution)/shard_map/ppermute | solution.py:234
  446.9 93.4 %collective-permute-start.14 = (bf16[2,256,2048]{2,1,0:T(8,128)(2,1)}, bf16[2,256,2048]{2,1,0:T(8,128)(2,1)}, u32[]{:S(2)}, u32[]{:S(2)}) collective-permute-start(bf16[2,256,2048]{2,1,0:T(8,128)(2,1)} %get-tuple-element.77.refs_16_), channel_id=1, source_target_pairs={{0,2},{1,3},{2,0},{3,1},{4,6},{5,7},{6,4},{7,5}} | collective-permute-start | bytes 6291464 | tf_op jit(solution)/shard_map/ppermute | solution.py:234
  448.6 92.3 %collective-permute-start.21 = (bf16[2,256,2048]{2,1,0:T(8,128)(2,1)}, bf16[2,256,2048]{2,1,0:T(8,128)(2,1)}, u32[]{:S(2)}, u32[]{:S(2)}) collective-permute-start(bf16[2,256,2048]{2,1,0:T(8,128)(2,1)} %get-tuple-element.88), channel_id=1, source_target_pairs={{0,4},{1,5},{2,6},{3,7},{4,0},{5,1},{6,2},{7,3}} | collective-permute-start | bytes 6291464 | tf_op jit(solution)/shard_map/ppermute | solution.py:234
  453.8 88.5 %collective-permute-start.19 = (bf16[2,256,2048]{2,1,0:T(8,128)(2,1)}, bf16[2,256,2048]{2,1,0:T(8,128)(2,1)}, u32[]{:S(2)}, u32[]{:S(2)}) collective-permute-start(bf16[2,256,2048]{2,1,0:T(8,128)(2,1)} %get-tuple-element.85), channel_id=1, source_target_pairs={{0,3},{1,2},{2,1},{3,0},{4,7},{5,6},{6,5},{7,4}} | collective-permute-start | bytes 6291464 | tf_op jit(solution)/shard_map/ppermute | solution.py:234
  538.7 75.3 %collective-permute-start.22 = (bf16[2,256,2048]{2,1,0:T(8,128)(2,1)}, bf16[2,256,2048]{2,1,0:T(8,128)(2,1)}, u32[]{:S(2)}, u32[]{:S(2)}) collective-permute-start(bf16[2,256,2048]{2,1,0:T(8,128)(2,1)} %get-tuple-element.89), channel_id=1, source_target_pairs={{0,5},{1,4},{2,7},{3,6},{4,1},{5,0},{6,3},{7,2}} | collective-permute-start | bytes 6291464 | tf_op jit(solution)/shard_map/ppermute | solution.py:234
  538.8 93.2 %collective-permute-start.40 = (f32[256,2048]{1,0:T(8,128)}, f32[256,2048]{1,0:T(8,128)}, u32[]{:S(2)}, u32[]{:S(2)}) collective-permute-start(f32[256,2048]{1,0:T(8,128)} %get-tuple-element.104.refs_8_), channel_id=1, source_target_pairs={{0,4},{1,5},{2,6},{3,7},{4,0},{5,1},{6,2},{7,3}} | collective-permute-start | bytes 6291464 | tf_op jit(solution)/shard_map/ppermute | solution.py:234
  540.3 91.7 %collective-permute-start.41 = (f32[256,2048]{1,0:T(8,128)}, f32[256,2048]{1,0:T(8,128)}, u32[]{:S(2)}, u32[]{:S(2)}) collective-permute-start(f32[256,2048]{1,0:T(8,128)} %get-tuple-element.107), channel_id=1, source_target_pairs={{0,2},{1,3},{2,0},{3,1},{4,6},{5,7},{6,4},{7,5}} | collective-permute-start | bytes 6291464 | tf_op jit(solution)/shard_map/ppermute | solution.py:234
  540.8 136.0 %collective-permute-start.38 = (f32[256,2048]{1,0:T(8,128)}, f32[256,2048]{1,0:T(8,128)}, u32[]{:S(2)}, u32[]{:S(2)}) collective-permute-start(f32[256,2048]{1,0:T(8,128)} %get-tuple-element.105.refs_15_), channel_id=1, source_target_pairs={{0,4},{1,5},{2,6},{3,7},{4,0},{5,1},{6,2},{7,3}} | collective-permute-start | bytes 6291464 | tf_op jit(solution)/shard_map/ppermute | solution.py:234
  542.3 134.6 %collective-permute-start.39 = (f32[256,2048]{1,0:T(8,128)}, f32[256,2048]{1,0:T(8,128)}, u32[]{:S(2)}, u32[]{:S(2)}) collective-permute-start(f32[256,2048]{1,0:T(8,128)} %get-tuple-element.106), channel_id=1, source_target_pairs={{0,2},{1,3},{2,0},{3,1},{4,6},{5,7},{6,4},{7,5}} | collective-permute-start | bytes 6291464 | tf_op jit(solution)/shard_map/ppermute | solution.py:234
  (18 other events, 605.8 us)
